TPU v7x, 32 devices: a whole 2x2x4 slice. The times are simulated.
32 devices in a mesh: groups: 2 (over y), seq: 4 (over z), blk: 2 (over x), tp: 2 (over core).
Axes of the slice: x: 2, y: 2, z: 4, core: 2. Of those that a mesh axis runs over, the one named last changes fastest.
Arguments:
- queries: bfloat16 [2048, 8192], P(('groups', 'seq', 'blk'), 'tp'), parts along dimension 0, may hold values from -160 to 160
- rotated_keys: bfloat16 [2048, 1024], P(('groups', 'seq', 'blk'), 'tp'), parts along dimension 0, may hold values from -5 to 5
- head_value_rows: bfloat16 [2048, 1024], P(('groups', 'seq', 'blk'), 'tp'), parts along dimension 0, may hold values from -6 to 6
- doc_lengths: int32 [16], P('groups'), parts along dimension 0, may hold values from 1 to 256, 1024 in all
- owner_plan: int32 [8, 2], P('groups'), parts along dimension 0, may hold values from 0 to 3, as said below
Outputs:
- attended: bfloat16 [4096, 8192], P(('groups', 'seq', 'blk'), 'tp'), parts along dimension 0
There are 2 independent parts, one for each index of `groups`. A program takes and returns all parts, laid end to end along the dimension named above; each array names one. Nothing has to cross between parts.
Inputs may be any that keep to these rules, and one draw needn't show every extreme that they name: `doc_lengths`: the lengths sum to 1024. `owner_plan`: group g consists of tokens g * 256 to g * 256 + 255, its block j of tokens j * 128 to j * 128 + 127 within the group. The entries of one row are distinct, so one group sends at most 1 block to one owner; in every draw some owner receives 1 block from every group.
All inputs are finite; a program needn't handle non-finite values.
Results may differ from a plain program's by a relative error of at most 0.0037.
Values may be sent and summed in bfloat16 or wider, within the bound.
No kernel may reach another device: no remote copies, remote signals or barrier semaphores. Data moves between devices by JAX's collectives and lax.ppermute only.
A program may use at most 64 MiB of HBM per device.

v0:
```python
import math

import jax
import jax.numpy as jnp
from jax import lax
from jax.experimental import pallas as pl
from jax.experimental.pallas import tpu as pltpu
from jax.sharding import PartitionSpec as P


QUERY_HEADS = 64
KEY_HEADS = 8
HEAD_WIDTH = 128
BLOCK = 128
HEADS_PER_GROUP = QUERY_HEADS // KEY_HEADS


masked_score = -1e30
exponent_scale = math.log2(math.e) / math.sqrt(HEAD_WIDTH)
vmem = pl.BlockSpec(memory_space=pltpu.VMEM)
smem = pl.BlockSpec(memory_space=pltpu.SMEM)
hbm = pl.BlockSpec(memory_space=pltpu.HBM)


def owner_of(step, group, blk, seq_count, block_axis):
    per_owner = seq_count // block_axis
    return (step + blk * per_owner + group % per_owner) % seq_count


def in_hbm(array):
    return pltpu.with_memory_space_constraint(array, pltpu.HBM)


def lanes(first, size):
    return pl.ds(pl.multiple_of(first, HEAD_WIDTH), size)


def kv_first(blk, dev_width):
    return blk * dev_width // (HEAD_WIDTH * HEADS_PER_GROUP) * HEAD_WIDTH


def pack_kernel(block_axis, dev_width, kv_width, chunks, query_ref, key_ref, value_ref, *refs):
    blk = lax.axis_index("blk")
    own_ref, prior_refs = refs[0], refs[1 : 1 + block_axis]
    rest, sems = refs[1 + block_axis : -1], refs[-1]
    moves = [(query_ref.at[:, lanes(blk * dev_width, dev_width)], own_ref)]
    for shift in range(block_axis):
        to = lax.rem(blk + shift, block_axis)
        kv = lanes(kv_first(to, dev_width), kv_width)
        targets = [prior_refs[shift]]
        for chunk, (first, size) in enumerate(chunks):
            if shift:
                out_ref = rest[chunk * (block_axis - 1) + shift - 1]
                columns = lanes(to * dev_width + first * HEAD_WIDTH, size * HEAD_WIDTH)
                if chunk == 0:
                    targets.append(out_ref)
                    out_ref = out_ref.at[:, pl.ds(2 * kv_width, size * HEAD_WIDTH)]
                moves.append((query_ref.at[:, columns], out_ref))
        for target in targets:
            moves.append((key_ref.at[:, kv], target.at[:, pl.ds(0, kv_width)]))
            moves.append((value_ref.at[:, kv], target.at[:, pl.ds(kv_width, kv_width)]))
    copies = [
        pltpu.make_async_copy(source, target, sems.at[index])
        for index, (source, target) in enumerate(moves)
    ]
    for copy in copies:
        copy.start()
    for copy in copies:
        copy.wait()


def attend_kernel(seq_count, block_axis, pair_room, kv_width, chunk, *refs):
    refs = list(refs)
    take = lambda count: [refs.pop(0) for _ in range(count)]
    doc_ref, plan_ref, own_query, own_kv = take(4)
    prior_refs = take(block_axis)
    home_refs = take(block_axis - 1)
    query_refs = take(block_axis - 1) if chunk[0] else home_refs
    message_refs = take(seq_count)
    query_all, key_all, value_all = refs
    group = lax.axis_index("seq")
    blk = lax.axis_index("blk")
    group_len = block_axis * BLOCK
    window = group_len + BLOCK
    first, heads = chunk
    columns = heads * HEAD_WIDTH
    query_at = 0 if first else 2 * kv_width
    kv_low = first // HEADS_PER_GROUP
    kv_high = (first + heads - 1) // HEADS_PER_GROUP + 1
    kv_from, kv_to = kv_low * HEAD_WIDTH, kv_high * HEAD_WIDTH
    doc_count = doc_ref.shape[0]

    for shift in range(block_axis):
        origin = lax.rem(blk - shift + block_axis, block_axis)
        rows = pl.ds(pl.multiple_of(origin * BLOCK, BLOCK), BLOCK)
        near_rows = pl.ds(pl.multiple_of(group_len + origin * BLOCK, BLOCK), BLOCK)
        if shift == 0:
            query = own_query[:, first * HEAD_WIDTH : first * HEAD_WIDTH + columns]
            home = own_kv
        else:
            query = query_refs[shift - 1][:, query_at : query_at + columns]
            home = home_refs[shift - 1]
        key_all[near_rows, :] = home[:, kv_from:kv_to]
        value_all[near_rows, :] = home[:, kv_width + kv_from : kv_width + kv_to]
        for head in range(heads):
            query_all[origin, head * BLOCK : (head + 1) * BLOCK, :] = query[
                :, head * HEAD_WIDTH : (head + 1) * HEAD_WIDTH
            ]
        key_all[rows, :] = prior_refs[shift][:, kv_from:kv_to]
        value_all[rows, :] = prior_refs[shift][:, kv_width + kv_from : kv_width + kv_to]

    def attend(block, out_ref, out_row):
        first_row = group * group_len + block * BLOCK
        query_pos = first_row + lax.broadcasted_iota(jnp.int32, (BLOCK, window), 0)
        key_pos = first_row - group_len + lax.broadcasted_iota(jnp.int32, (BLOCK, window), 1)
        row_pos = first_row + lax.broadcasted_iota(jnp.int32, (BLOCK, HEAD_WIDTH), 0)

        def reach(index, carried):
            end, start = carried
            end = end + doc_ref[index]
            return end, jnp.where(row_pos >= end, end, start)

        _, start = lax.fori_loop(
            0, doc_count, reach, (jnp.int32(0), jnp.zeros((BLOCK, HEAD_WIDTH), jnp.int32))
        )
        start = jnp.concatenate([start] * (window // HEAD_WIDTH), axis=1)
        allowed = (key_pos >= start) & (key_pos <= query_pos)
        key_rows = pl.ds(pl.multiple_of(block * BLOCK, BLOCK), window)
        for kv in range(kv_low, kv_high):
            low = max(first, kv * HEADS_PER_GROUP) - first
            high = min(first + heads, (kv + 1) * HEADS_PER_GROUP) - first
            kv_at = slice((kv - kv_low) * HEAD_WIDTH, (kv - kv_low + 1) * HEAD_WIDTH)
            scores = lax.dot_general(
                query_all[block, low * BLOCK : high * BLOCK, :],
                key_all[key_rows, kv_at],
                (((1,), (1,)), ((), ())),
                preferred_element_type=jnp.float32,
            )
            weights, totals = [], []
            for head in range(high - low):
                score = scores[head * BLOCK : (head + 1) * BLOCK]
                score = jnp.where(allowed, score, masked_score)
                top = jnp.max(score, axis=1, keepdims=True)
                weight = jnp.exp2((score - top) * exponent_scale)
                totals.append(jnp.sum(weight, axis=1, keepdims=True))
                weights.append(weight.astype(jnp.bfloat16))
            mixed = jnp.dot(
                jnp.concatenate(weights, axis=0),
                value_all[key_rows, kv_at],
                preferred_element_type=jnp.float32,
            )
            for head in range(high - low):
                at = slice((low + head) * HEAD_WIDTH, (low + head + 1) * HEAD_WIDTH)
                out_ref[out_row : out_row + BLOCK, at] = (
                    mixed[head * BLOCK : (head + 1) * BLOCK] / totals[head]
                ).astype(jnp.bfloat16)

    for step in range(seq_count):
        owner = owner_of(step, group, blk, seq_count, block_axis)
        for pair in range(pair_room):
            chosen = jnp.int32(-1)
            for block in range(plan_ref.shape[0]):
                chosen = jnp.where(
                    plan_ref[block, group] == owner * pair_room + pair, block, chosen
                )

            @pl.when(chosen >= 0)
            def _():
                attend(chosen, message_refs[step], pair * BLOCK)

            @pl.when(chosen < 0)
            def _():
                message_refs[step][pair * BLOCK : (pair + 1) * BLOCK, :] = jnp.zeros(
                    (BLOCK, columns), jnp.bfloat16
                )


def place_kernel(seq_count, block_axis, dev_width, first, *refs):
    messages = refs[:seq_count]
    out_ref, sems = refs[-2:]
    group = lax.axis_index("seq")
    per_owner = seq_count // block_axis
    rows, width = messages[0].shape
    copies = []
    for step in range(seq_count):
        origin = lax.rem(group - step + seq_count, seq_count)
        at_rows = pl.ds(pl.multiple_of(lax.rem(origin, per_owner) * rows, rows), rows)
        at_lanes = lanes(origin // per_owner * dev_width + first * HEAD_WIDTH, width)
        copies.append(
            pltpu.make_async_copy(messages[step], out_ref.at[at_rows, at_lanes], sems.at[step])
        )
    for copy in copies:
        copy.start()
    for copy in copies:
        copy.wait()


def per_device(queries, rotated_keys, head_value_rows, doc_lengths, owner_plan):
    block_axis = lax.axis_size("blk")
    seq_count = lax.axis_size("seq")
    local_tokens = queries.shape[0]
    group_blocks = local_tokens * block_axis // BLOCK
    heads_tp = queries.shape[1] // HEAD_WIDTH
    heads_dev = heads_tp // block_axis
    groups_kv = max(1, heads_dev // HEADS_PER_GROUP)
    dev_width = heads_dev * HEAD_WIDTH
    kv_width = groups_kv * HEAD_WIDTH
    pair_room = -(-2 * group_blocks // seq_count)
    per_owner = seq_count // block_axis
    slot_rows = pair_room * BLOCK
    window = (block_axis + 1) * BLOCK
    assert local_tokens == BLOCK and seq_count % block_axis == 0

    def permute(array, target):
        pairs = []
        for z in range(seq_count):
            for x in range(block_axis):
                to = target(z, x)
                if to is not None:
                    pairs.append((z * block_axis + x, to[0] * block_axis + to[1]))
        return lax.ppermute(array, ("seq", "blk"), pairs)

    head_counts = [heads_dev // 4, heads_dev - heads_dev // 4]
    chunks = [(sum(head_counts[:i]), count) for i, count in enumerate(head_counts)]

    bf16 = lambda *shape: jax.ShapeDtypeStruct(shape, jnp.bfloat16)
    peers = block_axis - 1
    out_shape = [bf16(BLOCK, dev_width)] + [bf16(BLOCK, 2 * kv_width)] * block_axis
    for first, size in chunks:
        out_shape += [bf16(BLOCK, size * HEAD_WIDTH + (0 if first else 2 * kv_width))] * peers
    own_query, *packed = pl.pallas_call(
        lambda *refs: pack_kernel(block_axis, dev_width, kv_width, chunks, *refs),
        out_shape=out_shape,
        in_specs=[hbm] * 3,
        out_specs=[vmem] * len(out_shape),
        scratch_shapes=[
            pltpu.SemaphoreType.DMA((1 + 2 * block_axis + peers * (2 + len(chunks)),))
        ],
        compiler_params=pltpu.CompilerParams(vmem_limit_bytes=8 << 20),
        name="pack",
    )(*map(in_hbm, (queries, rotated_keys, head_value_rows)))

    sideways = lambda shift: lambda z, x: (z, (x + shift) % block_axis)
    onward = lambda shift: lambda z, x: (
        (z + 1, (x + shift) % block_axis) if z + 1 < seq_count else None
    )
    home = [permute(packed[block_axis + s - 1], sideways(s)) for s in range(1, block_axis)]
    prior = [permute(packed[s], onward(s)) for s in range(block_axis)]
    later = [
        [permute(packed[block_axis + c * peers + s - 1], sideways(s)) for s in range(1, block_axis)]
        for c in range(1, len(chunks))
    ]

    out = None
    for index, chunk in enumerate(chunks):
        first, heads = chunk
        width = heads * HEAD_WIDTH
        kv_span = (
            (first + heads - 1) // HEADS_PER_GROUP + 1 - first // HEADS_PER_GROUP
        ) * HEAD_WIDTH
        inputs = [own_query, packed[0], *prior, *home]
        if index:
            inputs += later[index - 1]
        attend = pl.pallas_call(
            lambda *refs, chunk=chunk: attend_kernel(
                seq_count, block_axis, pair_room, kv_width, chunk, *refs
            ),
            out_shape=[bf16(slot_rows, width)] * seq_count,
            in_specs=[smem, smem] + [vmem] * len(inputs),
            out_specs=[vmem] * seq_count,
            scratch_shapes=[
                pltpu.VMEM((block_axis, heads * BLOCK, HEAD_WIDTH), jnp.bfloat16),
                pltpu.VMEM((2 * block_axis * BLOCK, kv_span), jnp.bfloat16),
                pltpu.VMEM((2 * block_axis * BLOCK, kv_span), jnp.bfloat16),
            ],
            cost_estimate=pl.CostEstimate(
                flops=8 * group_blocks * BLOCK * window * width,
                bytes_accessed=2 * seq_count * slot_rows * width,
                transcendentals=group_blocks * BLOCK * window * heads,
            ),
            compiler_params=pltpu.CompilerParams(vmem_limit_bytes=16 << 20),
        )
        messages = attend(in_hbm(doc_lengths), in_hbm(owner_plan.T), *inputs)
        arrived = [
            permute(
                messages[step],
                lambda z, x: (owner_of(step, z, x, seq_count, block_axis), z // per_owner),
            )
            for step in range(seq_count)
        ]
        carried = [] if out is None else [out]
        out = pl.pallas_call(
            lambda *refs, first=first: place_kernel(
                seq_count, block_axis, dev_width, first, *refs
            ),
            out_shape=bf16(per_owner * slot_rows, heads_tp * HEAD_WIDTH),
            in_specs=[vmem] * seq_count + [hbm] * len(carried),
            out_specs=hbm,
            scratch_shapes=[pltpu.SemaphoreType.DMA((seq_count,))],
            input_output_aliases={seq_count: 0} if carried else {},
            compiler_params=pltpu.CompilerParams(vmem_limit_bytes=8 << 20),
        )(*arrived, *carried)
    return out


def solution(mesh):
    in_specs = (
        P(("groups", "seq", "blk"), "tp"),
        P(("groups", "seq", "blk"), "tp"),
        P(("groups", "seq", "blk"), "tp"),
        P("groups"),
        P("groups", None),
    )
    out_specs = P(("groups", "seq", "blk"), "tp")

    return jax.shard_map(
        per_device, mesh=mesh, in_specs=in_specs, out_specs=out_specs, check_vma=False
    )
```

profile of v0, /device:TPU:2, one launch (start us, length us, event | category | flops | bytes accessed | tf_op | source)
XLA Modules:
  0.0 88.6 jit_solution(9672498051771131299)
XLA Ops:
  0.0 1.3 %pack.1 = (bf16[128,2048]{1,0:T(8,128)(2,1)S(1)}, bf16[128,512]{1,0:T(8,128)(2,1)S(1)}, bf16[128,512]{1,0:T(8,128)(2,1)S(1)}, bf16[128,1024]{1,0:T(8,128)(2,1)S(1)}, bf16[128,1536]{1,0:T(8,128)(2,1)S(1)}) custom-call(bf16[128,4096]{1,0:T(8,128)(2,1)} %refs_0_.3, bf16[128,512]{1,0:T(8,128)(2,1)} %refs_1_.1, bf16[128,512]{1,0:T(8,128)(2,1)} %refs_2_.1), custom_call_target="tpu_custom_call" | custom-call | tf_op jit(solution)/shard_map/pack/pallas_call | solution.py:231
  1.3 0.1 collective-permute-start.3
  1.4 2.0 %collective-permute-start.2 = (bf16[128,1024]{1,0:T(8,128)(2,1)S(1)}, bf16[128,1024]{1,0:T(8,128)(2,1)S(1)}, u32[]{:S(2)}, u32[]{:S(2)}) collective-permute-start(bf16[128,1024]{1,0:T(8,128)(2,1)S(1)} %get-tuple-element.21), channel_id=1, source_target_pairs={{0,2},{2,0},{4,6},{6,4},{8,10},{10,8},{12,14},{14,12},{1,3},{3,1},... | collective-permute-start | bytes 786440 | tf_op jit(solution)/shard_map/ppermute | solution.py:221
  3.4 3.4 %collective-permute-start.1 = (bf16[128,512]{1,0:T(8,128)(2,1)S(1)}, bf16[128,512]{1,0:T(8,128)(2,1)S(1)}, u32[]{:S(2)}, u32[]{:S(2)}) collective-permute-start(bf16[128,512]{1,0:T(8,128)(2,1)S(1)} %get-tuple-element.20), channel_id=1, source_target_pairs={{0,6},{2,4},{4,10},{6,8},{8,14},{10,12},{1,7},{3,5},{5,11},{7,9},{... | collective-permute-start | bytes 393224 | tf_op jit(solution)/shard_map/ppermute | solution.py:221
  6.9 3.5 %collective-permute-start = (bf16[128,512]{1,0:T(8,128)(2,1)S(1)}, bf16[128,512]{1,0:T(8,128)(2,1)S(1)}, u32[]{:S(2)}, u32[]{:S(2)}) collective-permute-start(bf16[128,512]{1,0:T(8,128)(2,1)S(1)} %get-tuple-element.19.refs_3_), channel_id=1, source_target_pairs={{0,4},{2,6},{4,8},{6,10},{8,12},{10,14},{1,5},{3,7},{5,9},{7,11},{... | collective-permute-start | bytes 393224 | tf_op jit(solution)/shard_map/ppermute | solution.py:221
  10.4 2.5 %collective-permute-done.refs_4_ = bf16[128,512]{1,0:T(8,128)(2,1)S(1)} collective-permute-done((bf16[128,512]{1,0:T(8,128)(2,1)S(1)}, bf16[128,512]{1,0:T(8,128)(2,1)S(1)}, u32[]{:S(2)}, u32[]{:S(2)}) %collective-permute-start) | collective-permute-done | bytes 131104 | tf_op jit(solution)/shard_map/ppermute | solution.py:221
  12.9 5.0 %collective-permute-done.2.refs_6_ = bf16[128,1024]{1,0:T(8,128)(2,1)S(1)} collective-permute-done((bf16[128,1024]{1,0:T(8,128)(2,1)S(1)}, bf16[128,1024]{1,0:T(8,128)(2,1)S(1)}, u32[]{:S(2)}, u32[]{:S(2)}) %collective-permute-start.2) | collective-permute-done | bytes 262176 | tf_op jit(solution)/shard_map/ppermute | solution.py:221
  17.9 2.1 %shard_map.56 = (bf16[128,512]{1,0:T(8,128)(2,1)S(1)}, bf16[128,512]{1,0:T(8,128)(2,1)S(1)}, bf16[128,512]{1,0:T(8,128)(2,1)S(1)}, bf16[128,512]{1,0:T(8,128)(2,1)S(1)}) custom-call(s32[8]{0:T(128)} %refs_0_.5, s32[2,4]{1,0:T(2,128)} %bitcast.1, bf16[128,2048]{1,0:T(8,128)(2,1)S(1)} %get-tuple-element.18.refs_2_, ...), custom_call_target="tpu_custom_call" | custom-call | flops 402653184 | bytes 524288 | tf_op jit(solution)/shard_map/pallas_call | solution.py:283
  20.0 7.3 %collective-permute-start.8 = (bf16[128,512]{1,0:T(8,128)(2,1)S(1)}, bf16[128,512]{1,0:T(8,128)(2,1)S(1)}, u32[]{:S(2)}, u32[]{:S(2)}) collective-permute-start(bf16[128,512]{1,0:T(8,128)(2,1)S(1)} %get-tuple-element.27), channel_id=1, source_target_pairs={{0,0},{2,8},{4,4},{6,12},{8,2},{10,10},{12,6},{14,14},{1,1},{3,9},... | collective-permute-start | bytes 393224 | tf_op jit(solution)/shard_map/ppermute | solution.py:221
  27.3 2.3 %collective-permute-start.9 = (bf16[128,512]{1,0:T(8,128)(2,1)S(1)}, bf16[128,512]{1,0:T(8,128)(2,1)S(1)}, u32[]{:S(2)}, u32[]{:S(2)}) collective-permute-start(bf16[128,512]{1,0:T(8,128)(2,1)S(1)} %get-tuple-element.28), channel_id=1, source_target_pairs={{0,4},{2,12},{4,8},{6,0},{8,6},{10,14},{12,10},{14,2},{1,5},{3,13}... | collective-permute-start | bytes 393224 | tf_op jit(solution)/shard_map/ppermute | solution.py:221
  29.6 0.0 collective-permute-done.3.refs_7_
  29.6 3.3 %shard_map.55 = (bf16[128,1536]{1,0:T(8,128)(2,1)S(1)}, bf16[128,1536]{1,0:T(8,128)(2,1)S(1)}, bf16[128,1536]{1,0:T(8,128)(2,1)S(1)}, bf16[128,1536]{1,0:T(8,128)(2,1)S(1)}) custom-call(s32[8]{0:T(128)} %refs_0_.5, s32[2,4]{1,0:T(2,128)} %bitcast.2, bf16[128,2048]{1,0:T(8,128)(2,1)S(1)} %get-tuple-element.18.refs_2_, ...), custom_call_target="tpu_custom_call" | custom-call | flops 1207959552 | bytes 1572864 | tf_op jit(solution)/shard_map/pallas_call | solution.py:283
  32.9 3.6 %collective-permute-start.4 = (bf16[128,1536]{1,0:T(8,128)(2,1)S(1)}, bf16[128,1536]{1,0:T(8,128)(2,1)S(1)}, u32[]{:S(2)}, u32[]{:S(2)}) collective-permute-start(bf16[128,1536]{1,0:T(8,128)(2,1)S(1)} %get-tuple-element.23), channel_id=1, source_target_pairs={{0,0},{2,8},{4,4},{6,12},{8,2},{10,10},{12,6},{14,14},{1,1},{3,9},... | collective-permute-start | bytes 1179656 | tf_op jit(solution)/shard_map/ppermute | solution.py:221
  36.5 1.0 %collective-permute-start.5 = (bf16[128,1536]{1,0:T(8,128)(2,1)S(1)}, bf16[128,1536]{1,0:T(8,128)(2,1)S(1)}, u32[]{:S(2)}, u32[]{:S(2)}) collective-permute-start(bf16[128,1536]{1,0:T(8,128)(2,1)S(1)} %get-tuple-element.24), channel_id=1, source_target_pairs={{0,4},{2,12},{4,8},{6,0},{8,6},{10,14},{12,10},{14,2},{1,5},{3,13}... | collective-permute-start | bytes 1179656 | tf_op jit(solution)/shard_map/ppermute | solution.py:221
  37.5 0.0 collective-permute-start.6
  37.5 1.8 %collective-permute-start.7 = (bf16[128,1536]{1,0:T(8,128)(2,1)S(1)}, bf16[128,1536]{1,0:T(8,128)(2,1)S(1)}, u32[]{:S(2)}, u32[]{:S(2)}) collective-permute-start(bf16[128,1536]{1,0:T(8,128)(2,1)S(1)} %get-tuple-element.26), channel_id=1, source_target_pairs={{0,12},{2,4},{4,0},{6,8},{8,14},{10,6},{12,2},{14,10},{1,13},{3,5}... | collective-permute-start | bytes 1179656 | tf_op jit(solution)/shard_map/ppermute | solution.py:221
  39.3 16.6 %collective-permute-start.10 = (bf16[128,512]{1,0:T(8,128)(2,1)S(1)}, bf16[128,512]{1,0:T(8,128)(2,1)S(1)}, u32[]{:S(2)}, u32[]{:S(2)}) collective-permute-start(bf16[128,512]{1,0:T(8,128)(2,1)S(1)} %get-tuple-element.29), channel_id=1, source_target_pairs={{0,8},{2,0},{4,12},{6,4},{8,10},{10,2},{12,14},{14,6},{1,9},{3,1},... | collective-permute-start | bytes 393224 | tf_op jit(solution)/shard_map/ppermute | solution.py:221
  55.9 22.6 %collective-permute-done.10.refs_2_ = bf16[128,512]{1,0:T(8,128)(2,1)S(1)} collective-permute-done((bf16[128,512]{1,0:T(8,128)(2,1)S(1)}, bf16[128,512]{1,0:T(8,128)(2,1)S(1)}, u32[]{:S(2)}, u32[]{:S(2)}) %collective-permute-start.10) | collective-permute-done | bytes 131104 | tf_op jit(solution)/shard_map/ppermute | solution.py:221
  78.5 0.0 collective-permute-start.11
  78.5 8.1 %collective-permute-done.11.refs_3_ = bf16[128,512]{1,0:T(8,128)(2,1)S(1)} collective-permute-done((bf16[128,512]{1,0:T(8,128)(2,1)S(1)}, bf16[128,512]{1,0:T(8,128)(2,1)S(1)}, u32[]{:S(2)}, u32[]{:S(2)}) %collective-permute-start.11) | collective-permute-done | bytes 131104 | tf_op jit(solution)/shard_map/ppermute | solution.py:221
  86.6 0.8 shard_map.57.refs_4_
  87.4 0.0 collective-permute-done.4.refs_0_
  87.4 0.0 collective-permute-done.5.refs_1_
  87.4 1.2 %shard_map.58 = bf16[256,4096]{1,0:T(8,128)(2,1)} custom-call(bf16[128,1536]{1,0:T(8,128)(2,1)S(1)} %collective-permute-done.4.refs_0_, bf16[128,1536]{1,0:T(8,128)(2,1)S(1)} %collective-permute-done.5.refs_1_, bf16[128,1536]{1,0:T(8,128)(2,1)S(1)} %collective-permute-done.6.refs_2_, ...), custom_call_target="tpu_custom_call", output_to_operand_aliasing={{}: (4, {})} | custom-call | tf_op jit(solution)/shard_map/pallas_call | solution.py:292
  (5 shorter events, 0.0 us)
Async XLA Ops:
  1.3 28.3 %collective-permute-start.3 = (bf16[128,1536]{1,0:T(8,128)(2,1)S(1)}, bf16[128,1536]{1,0:T(8,128)(2,1)S(1)}, u32[]{:S(2)}, u32[]{:S(2)}) collective-permute-start(bf16[128,1536]{1,0:T(8,128)(2,1)S(1)} %get-tuple-element.22), channel_id=1, source_target_pairs={{0,2},{2,0},{4,6},{6,4},{8,10},{10,8},{12,14},{14,12},{1,3},{3,1},... | collective-permute-start | bytes 1179656 | tf_op jit(solution)/shard_map/ppermute | solution.py:221
  1.4 16.5 %collective-permute-start.2 = (bf16[128,1024]{1,0:T(8,128)(2,1)S(1)}, bf16[128,1024]{1,0:T(8,128)(2,1)S(1)}, u32[]{:S(2)}, u32[]{:S(2)}) collective-permute-start(bf16[128,1024]{1,0:T(8,128)(2,1)S(1)} %get-tuple-element.21), channel_id=1, source_target_pairs={{0,2},{2,0},{4,6},{6,4},{8,10},{10,8},{12,14},{14,12},{1,3},{3,1},... | collective-permute-start | bytes 786440 | tf_op jit(solution)/shard_map/ppermute | solution.py:221
  3.4 7.0 %collective-permute-start.1 = (bf16[128,512]{1,0:T(8,128)(2,1)S(1)}, bf16[128,512]{1,0:T(8,128)(2,1)S(1)}, u32[]{:S(2)}, u32[]{:S(2)}) collective-permute-start(bf16[128,512]{1,0:T(8,128)(2,1)S(1)} %get-tuple-element.20), channel_id=1, source_target_pairs={{0,6},{2,4},{4,10},{6,8},{8,14},{10,12},{1,7},{3,5},{5,11},{7,9},{... | collective-permute-start | bytes 393224 | tf_op jit(solution)/shard_map/ppermute | solution.py:221
  6.9 6.0 %collective-permute-start = (bf16[128,512]{1,0:T(8,128)(2,1)S(1)}, bf16[128,512]{1,0:T(8,128)(2,1)S(1)}, u32[]{:S(2)}, u32[]{:S(2)}) collective-permute-start(bf16[128,512]{1,0:T(8,128)(2,1)S(1)} %get-tuple-element.19.refs_3_), channel_id=1, source_target_pairs={{0,4},{2,6},{4,8},{6,10},{8,12},{10,14},{1,5},{3,7},{5,9},{7,11},{... | collective-permute-start | bytes 393224 | tf_op jit(solution)/shard_map/ppermute | solution.py:221
  20.0 17.5 %collective-permute-start.8 = (bf16[128,512]{1,0:T(8,128)(2,1)S(1)}, bf16[128,512]{1,0:T(8,128)(2,1)S(1)}, u32[]{:S(2)}, u32[]{:S(2)}) collective-permute-start(bf16[128,512]{1,0:T(8,128)(2,1)S(1)} %get-tuple-element.27), channel_id=1, source_target_pairs={{0,0},{2,8},{4,4},{6,12},{8,2},{10,10},{12,6},{14,14},{1,1},{3,9},... | collective-permute-start | bytes 393224 | tf_op jit(solution)/shard_map/ppermute | solution.py:221
  27.3 12.0 %collective-permute-start.9 = (bf16[128,512]{1,0:T(8,128)(2,1)S(1)}, bf16[128,512]{1,0:T(8,128)(2,1)S(1)}, u32[]{:S(2)}, u32[]{:S(2)}) collective-permute-start(bf16[128,512]{1,0:T(8,128)(2,1)S(1)} %get-tuple-element.28), channel_id=1, source_target_pairs={{0,4},{2,12},{4,8},{6,0},{8,6},{10,14},{12,10},{14,2},{1,5},{3,13}... | collective-permute-start | bytes 393224 | tf_op jit(solution)/shard_map/ppermute | solution.py:221
  32.9 54.5 %collective-permute-start.4 = (bf16[128,1536]{1,0:T(8,128)(2,1)S(1)}, bf16[128,1536]{1,0:T(8,128)(2,1)S(1)}, u32[]{:S(2)}, u32[]{:S(2)}) collective-permute-start(bf16[128,1536]{1,0:T(8,128)(2,1)S(1)} %get-tuple-element.23), channel_id=1, source_target_pairs={{0,0},{2,8},{4,4},{6,12},{8,2},{10,10},{12,6},{14,14},{1,1},{3,9},... | collective-permute-start | bytes 1179656 | tf_op jit(solution)/shard_map/ppermute | solution.py:221
  36.5 50.9 %collective-permute-start.5 = (bf16[128,1536]{1,0:T(8,128)(2,1)S(1)}, bf16[128,1536]{1,0:T(8,128)(2,1)S(1)}, u32[]{:S(2)}, u32[]{:S(2)}) collective-permute-start(bf16[128,1536]{1,0:T(8,128)(2,1)S(1)} %get-tuple-element.24), channel_id=1, source_target_pairs={{0,4},{2,12},{4,8},{6,0},{8,6},{10,14},{12,10},{14,2},{1,5},{3,13}... | collective-permute-start | bytes 1179656 | tf_op jit(solution)/shard_map/ppermute | solution.py:221
  37.5 49.9 %collective-permute-start.6 = (bf16[128,1536]{1,0:T(8,128)(2,1)S(1)}, bf16[128,1536]{1,0:T(8,128)(2,1)S(1)}, u32[]{:S(2)}, u32[]{:S(2)}) collective-permute-start(bf16[128,1536]{1,0:T(8,128)(2,1)S(1)} %get-tuple-element.25), channel_id=1, source_target_pairs={{0,8},{2,0},{4,12},{6,4},{8,10},{10,2},{12,14},{14,6},{1,9},{3,1},... | collective-permute-start | bytes 1179656 | tf_op jit(solution)/shard_map/ppermute | solution.py:221
  37.5 49.9 %collective-permute-start.7 = (bf16[128,1536]{1,0:T(8,128)(2,1)S(1)}, bf16[128,1536]{1,0:T(8,128)(2,1)S(1)}, u32[]{:S(2)}, u32[]{:S(2)}) collective-permute-start(bf16[128,1536]{1,0:T(8,128)(2,1)S(1)} %get-tuple-element.26), channel_id=1, source_target_pairs={{0,12},{2,4},{4,0},{6,8},{8,14},{10,6},{12,2},{14,10},{1,13},{3,5}... | collective-permute-start | bytes 1179656 | tf_op jit(solution)/shard_map/ppermute | solution.py:221
  39.3 39.2 %collective-permute-start.10 = (bf16[128,512]{1,0:T(8,128)(2,1)S(1)}, bf16[128,512]{1,0:T(8,128)(2,1)S(1)}, u32[]{:S(2)}, u32[]{:S(2)}) collective-permute-start(bf16[128,512]{1,0:T(8,128)(2,1)S(1)} %get-tuple-element.29), channel_id=1, source_target_pairs={{0,8},{2,0},{4,12},{6,4},{8,10},{10,2},{12,14},{14,6},{1,9},{3,1},... | collective-permute-start | bytes 393224 | tf_op jit(solution)/shard_map/ppermute | solution.py:221
  78.5 8.1 %collective-permute-start.11 = (bf16[128,512]{1,0:T(8,128)(2,1)S(1)}, bf16[128,512]{1,0:T(8,128)(2,1)S(1)}, u32[]{:S(2)}, u32[]{:S(2)}) collective-permute-start(bf16[128,512]{1,0:T(8,128)(2,1)S(1)} %get-tuple-element.30), channel_id=1, source_target_pairs={{0,12},{2,4},{4,0},{6,8},{8,14},{10,6},{12,2},{14,10},{1,13},{3,5}... | collective-permute-start | bytes 393224 | tf_op jit(solution)/shard_map/ppermute | solution.py:221
where the time goes:
time: 88.9 us; the launch traced here: 88.6 us
  starting transfers between devices  41.6 us (47%)
  waiting for transfers between devices  38.2 us (43%)
  Pallas kernels  8.77 us (10%)
    ppermute x12, starting transfers between devices, permute(): return lax.ppermute(array, ('seq', 'blk'), pairs)  41.6 us
    ppermute x12, waiting for transfers between devices, permute(): return lax.ppermute(array, ('seq', 'blk'), pairs)  38.2 us
    pallas_call x2, Pallas kernels, per_device(): messages = attend(in_hbm(doc_lengths), in_hbm(owner_plan.T), *inputs)  5.42 us
    pallas_call x2, Pallas kernels, per_device(): pl.pallas_call(lambda *refs, first=first: place_kernel(seq_count, block_a...  2.01 us
  transfers between devices with their start and end apart: 12, of which 4 were waited for; matrix products, arithmetic and copies ran while one was open for 0% of the time, Pallas kernels for 7%

commit v1 on v0

--- a/solution.py
+++ b/solution.py
@@ -23,8 +23,7 @@
 
 
 def owner_of(step, group, blk, seq_count, block_axis):
-    per_owner = seq_count // block_axis
-    return (step + blk * per_owner + group % per_owner) % seq_count
+    return group ^ step ^ (blk * (seq_count // block_axis))
 
 
 def in_hbm(array):
@@ -179,11 +178,12 @@
     messages = refs[:seq_count]
     out_ref, sems = refs[-2:]
     group = lax.axis_index("seq")
+    blk = lax.axis_index("blk")
     per_owner = seq_count // block_axis
     rows, width = messages[0].shape
     copies = []
     for step in range(seq_count):
-        origin = lax.rem(group - step + seq_count, seq_count)
+        origin = group ^ step ^ (blk * per_owner)
         at_rows = pl.ds(pl.multiple_of(lax.rem(origin, per_owner) * rows, rows), rows)
         at_lanes = lanes(origin // per_owner * dev_width + first * HEAD_WIDTH, width)
         copies.append(
@@ -210,14 +210,14 @@
     slot_rows = pair_room * BLOCK
     window = (block_axis + 1) * BLOCK
     assert local_tokens == BLOCK and seq_count % block_axis == 0
+    assert seq_count & (seq_count - 1) == 0 and block_axis & (block_axis - 1) == 0
 
     def permute(array, target):
         pairs = []
         for z in range(seq_count):
             for x in range(block_axis):
                 to = target(z, x)
-                if to is not None:
-                    pairs.append((z * block_axis + x, to[0] * block_axis + to[1]))
+                pairs.append((z * block_axis + x, to[0] * block_axis + to[1]))
         return lax.ppermute(array, ("seq", "blk"), pairs)
 
     head_counts = [heads_dev // 4, heads_dev - heads_dev // 4]
@@ -241,9 +241,7 @@
     )(*map(in_hbm, (queries, rotated_keys, head_value_rows)))
 
     sideways = lambda shift: lambda z, x: (z, (x + shift) % block_axis)
-    onward = lambda shift: lambda z, x: (
-        (z + 1, (x + shift) % block_axis) if z + 1 < seq_count else None
-    )
+    onward = lambda shift: lambda z, x: ((z + 1) % seq_count, (x + shift) % block_axis)
     home = [permute(packed[block_axis + s - 1], sideways(s)) for s in range(1, block_axis)]
     prior = [permute(packed[s], onward(s)) for s in range(block_axis)]
     later = [

time: 88.9 us -> 92.7 us (1.043)
  waiting for transfers between devices: 38.2 us -> 57.6 us
  starting transfers between devices: 41.6 us -> 26 us
    ppermute x12, waiting for transfers between devices: 38.2 us -> 57.6 us  [permute(): return lax.ppermute(array, ('seq', 'blk'), pairs)]
    ppermute x12, starting transfers between devices: 41.6 us -> 26 us  [permute(): return lax.ppermute(array, ('seq', 'blk'), pairs)]
  transfers between devices with their start and end apart: 12 -> 12, of which waited for: 4 -> 6; matrix products, arithmetic and copies ran while one was open for 0% -> 0% of each run, Pallas kernels for 7% -> 7%
where the time goes in v1:
time: 92.7 us; the launch traced here: 92.5 us
  waiting for transfers between devices  57.6 us (62%)
  starting transfers between devices  26 us (28%)
  Pallas kernels  8.76 us (9%)
    ppermute x12, waiting for transfers between devices, permute(): return lax.ppermute(array, ('seq', 'blk'), pairs)  57.6 us
    ppermute x12, starting transfers between devices, permute(): return lax.ppermute(array, ('seq', 'blk'), pairs)  26 us
    pallas_call x2, Pallas kernels, per_device(): messages = attend(in_hbm(doc_lengths), in_hbm(owner_plan.T), *inputs)  5.41 us
    pallas_call x2, Pallas kernels, per_device(): pl.pallas_call(lambda *refs, first=first: place_kernel(seq_count, block_a...  2.01 us
  transfers between devices with their start and end apart: 12, of which 6 were waited for; matrix products, arithmetic and copies ran while one was open for 0% of the time, Pallas kernels for 7%

profile of v1, /device:TPU:2, one launch (start us, length us, event | category | flops | bytes accessed | tf_op | source)
XLA Modules:
  0.0 92.5 jit_solution(18310399910667423078)
XLA Ops:
  0.0 1.3 %pack.1 = (bf16[128,2048]{1,0:T(8,128)(2,1)S(1)}, bf16[128,512]{1,0:T(8,128)(2,1)S(1)}, bf16[128,512]{1,0:T(8,128)(2,1)S(1)}, bf16[128,1024]{1,0:T(8,128)(2,1)S(1)}, bf16[128,1536]{1,0:T(8,128)(2,1)S(1)}) custom-call(bf16[128,4096]{1,0:T(8,128)(2,1)} %refs_0_.3, bf16[128,512]{1,0:T(8,128)(2,1)} %refs_1_.1, bf16[128,512]{1,0:T(8,128)(2,1)} %refs_2_.1), custom_call_target="tpu_custom_call" | custom-call | tf_op jit(solution)/shard_map/pack/pallas_call | solution.py:231
  1.3 0.1 collective-permute-start.3
  1.4 2.0 %collective-permute-start.2 = (bf16[128,1024]{1,0:T(8,128)(2,1)S(1)}, bf16[128,1024]{1,0:T(8,128)(2,1)S(1)}, u32[]{:S(2)}, u32[]{:S(2)}) collective-permute-start(bf16[128,1024]{1,0:T(8,128)(2,1)S(1)} %get-tuple-element.21), channel_id=1, source_target_pairs={{0,2},{2,0},{4,6},{6,4},{8,10},{10,8},{12,14},{14,12},{1,3},{3,1},... | collective-permute-start | bytes 786440 | tf_op jit(solution)/shard_map/ppermute | solution.py:221
  3.4 1.5 %collective-permute-start.1 = (bf16[128,512]{1,0:T(8,128)(2,1)S(1)}, bf16[128,512]{1,0:T(8,128)(2,1)S(1)}, u32[]{:S(2)}, u32[]{:S(2)}) collective-permute-start(bf16[128,512]{1,0:T(8,128)(2,1)S(1)} %get-tuple-element.20), channel_id=1, source_target_pairs={{0,6},{2,4},{4,10},{6,8},{8,14},{10,12},{12,2},{14,0},{1,7},{3,5},... | collective-permute-start | bytes 393224 | tf_op jit(solution)/shard_map/ppermute | solution.py:221
  5.0 1.6 %collective-permute-start = (bf16[128,512]{1,0:T(8,128)(2,1)S(1)}, bf16[128,512]{1,0:T(8,128)(2,1)S(1)}, u32[]{:S(2)}, u32[]{:S(2)}) collective-permute-start(bf16[128,512]{1,0:T(8,128)(2,1)S(1)} %get-tuple-element.19.refs_3_), channel_id=1, source_target_pairs={{0,4},{2,6},{4,8},{6,10},{8,12},{10,14},{12,0},{14,2},{1,5},{3,7},... | collective-permute-start | bytes 393224 | tf_op jit(solution)/shard_map/ppermute | solution.py:221
  6.6 5.7 %collective-permute-done.1.refs_5_ = bf16[128,512]{1,0:T(8,128)(2,1)S(1)} collective-permute-done((bf16[128,512]{1,0:T(8,128)(2,1)S(1)}, bf16[128,512]{1,0:T(8,128)(2,1)S(1)}, u32[]{:S(2)}, u32[]{:S(2)}) %collective-permute-start.1) | collective-permute-done | bytes 131104 | tf_op jit(solution)/shard_map/ppermute | solution.py:221
  12.3 0.6 collective-permute-done.refs_4_
  12.8 7.9 %collective-permute-done.2.refs_6_ = bf16[128,1024]{1,0:T(8,128)(2,1)S(1)} collective-permute-done((bf16[128,1024]{1,0:T(8,128)(2,1)S(1)}, bf16[128,1024]{1,0:T(8,128)(2,1)S(1)}, u32[]{:S(2)}, u32[]{:S(2)}) %collective-permute-start.2) | collective-permute-done | bytes 262176 | tf_op jit(solution)/shard_map/ppermute | solution.py:221
  20.7 2.1 %shard_map.56 = (bf16[128,512]{1,0:T(8,128)(2,1)S(1)}, bf16[128,512]{1,0:T(8,128)(2,1)S(1)}, bf16[128,512]{1,0:T(8,128)(2,1)S(1)}, bf16[128,512]{1,0:T(8,128)(2,1)S(1)}) custom-call(s32[8]{0:T(128)} %refs_0_.5, s32[2,4]{1,0:T(2,128)} %bitcast.1, bf16[128,2048]{1,0:T(8,128)(2,1)S(1)} %get-tuple-element.18.refs_2_, ...), custom_call_target="tpu_custom_call" | custom-call | flops 402653184 | bytes 524288 | tf_op jit(solution)/shard_map/pallas_call | solution.py:281
  22.8 4.5 %collective-permute-start.8 = (bf16[128,512]{1,0:T(8,128)(2,1)S(1)}, bf16[128,512]{1,0:T(8,128)(2,1)S(1)}, u32[]{:S(2)}, u32[]{:S(2)}) collective-permute-start(bf16[128,512]{1,0:T(8,128)(2,1)S(1)} %get-tuple-element.27), channel_id=1, source_target_pairs={{0,0},{2,8},{4,4},{6,12},{8,10},{10,2},{12,14},{14,6},{1,1},{3,9},... | collective-permute-start | bytes 393224 | tf_op jit(solution)/shard_map/ppermute | solution.py:221
  27.3 2.6 %collective-permute-start.9 = (bf16[128,512]{1,0:T(8,128)(2,1)S(1)}, bf16[128,512]{1,0:T(8,128)(2,1)S(1)}, u32[]{:S(2)}, u32[]{:S(2)}) collective-permute-start(bf16[128,512]{1,0:T(8,128)(2,1)S(1)} %get-tuple-element.28), channel_id=1, source_target_pairs={{0,4},{2,12},{4,0},{6,8},{8,14},{10,6},{12,10},{14,2},{1,5},{3,13}... | collective-permute-start | bytes 393224 | tf_op jit(solution)/shard_map/ppermute | solution.py:221
  29.8 0.0 collective-permute-done.3.refs_7_
  29.8 3.3 %shard_map.55 = (bf16[128,1536]{1,0:T(8,128)(2,1)S(1)}, bf16[128,1536]{1,0:T(8,128)(2,1)S(1)}, bf16[128,1536]{1,0:T(8,128)(2,1)S(1)}, bf16[128,1536]{1,0:T(8,128)(2,1)S(1)}) custom-call(s32[8]{0:T(128)} %refs_0_.5, s32[2,4]{1,0:T(2,128)} %bitcast.2, bf16[128,2048]{1,0:T(8,128)(2,1)S(1)} %get-tuple-element.18.refs_2_, ...), custom_call_target="tpu_custom_call" | custom-call | flops 1207959552 | bytes 1572864 | tf_op jit(solution)/shard_map/pallas_call | solution.py:281
  33.2 2.2 %collective-permute-start.4 = (bf16[128,1536]{1,0:T(8,128)(2,1)S(1)}, bf16[128,1536]{1,0:T(8,128)(2,1)S(1)}, u32[]{:S(2)}, u32[]{:S(2)}) collective-permute-start(bf16[128,1536]{1,0:T(8,128)(2,1)S(1)} %get-tuple-element.23), channel_id=1, source_target_pairs={{0,0},{2,8},{4,4},{6,12},{8,10},{10,2},{12,14},{14,6},{1,1},{3,9},... | collective-permute-start | bytes 1179656 | tf_op jit(solution)/shard_map/ppermute | solution.py:221
  35.4 2.5 %collective-permute-start.5 = (bf16[128,1536]{1,0:T(8,128)(2,1)S(1)}, bf16[128,1536]{1,0:T(8,128)(2,1)S(1)}, u32[]{:S(2)}, u32[]{:S(2)}) collective-permute-start(bf16[128,1536]{1,0:T(8,128)(2,1)S(1)} %get-tuple-element.24), channel_id=1, source_target_pairs={{0,4},{2,12},{4,0},{6,8},{8,14},{10,6},{12,10},{14,2},{1,5},{3,13}... | collective-permute-start | bytes 1179656 | tf_op jit(solution)/shard_map/ppermute | solution.py:221
  37.9 1.9 %collective-permute-start.6 = (bf16[128,1536]{1,0:T(8,128)(2,1)S(1)}, bf16[128,1536]{1,0:T(8,128)(2,1)S(1)}, u32[]{:S(2)}, u32[]{:S(2)}) collective-permute-start(bf16[128,1536]{1,0:T(8,128)(2,1)S(1)} %get-tuple-element.25), channel_id=1, source_target_pairs={{0,8},{2,0},{4,12},{6,4},{8,2},{10,10},{12,6},{14,14},{1,9},{3,1},... | collective-permute-start | bytes 1179656 | tf_op jit(solution)/shard_map/ppermute | solution.py:221
  39.8 11.9 %collective-permute-done.8.refs_0_ = bf16[128,512]{1,0:T(8,128)(2,1)S(1)} collective-permute-done((bf16[128,512]{1,0:T(8,128)(2,1)S(1)}, bf16[128,512]{1,0:T(8,128)(2,1)S(1)}, u32[]{:S(2)}, u32[]{:S(2)}) %collective-permute-start.8) | collective-permute-done | bytes 131104 | tf_op jit(solution)/shard_map/ppermute | solution.py:221
  51.8 7.1 %collective-permute-start.10 = (bf16[128,512]{1,0:T(8,128)(2,1)S(1)}, bf16[128,512]{1,0:T(8,128)(2,1)S(1)}, u32[]{:S(2)}, u32[]{:S(2)}) collective-permute-start(bf16[128,512]{1,0:T(8,128)(2,1)S(1)} %get-tuple-element.29), channel_id=1, source_target_pairs={{0,8},{2,0},{4,12},{6,4},{8,2},{10,10},{12,6},{14,14},{1,9},{3,1},... | collective-permute-start | bytes 393224 | tf_op jit(solution)/shard_map/ppermute | solution.py:221
  58.9 23.9 %collective-permute-done.10.refs_2_ = bf16[128,512]{1,0:T(8,128)(2,1)S(1)} collective-permute-done((bf16[128,512]{1,0:T(8,128)(2,1)S(1)}, bf16[128,512]{1,0:T(8,128)(2,1)S(1)}, u32[]{:S(2)}, u32[]{:S(2)}) %collective-permute-start.10) | collective-permute-done | bytes 131104 | tf_op jit(solution)/shard_map/ppermute | solution.py:221
  82.8 7.7 %collective-permute-done.11.refs_3_ = bf16[128,512]{1,0:T(8,128)(2,1)S(1)} collective-permute-done((bf16[128,512]{1,0:T(8,128)(2,1)S(1)}, bf16[128,512]{1,0:T(8,128)(2,1)S(1)}, u32[]{:S(2)}, u32[]{:S(2)}) %collective-permute-start.11) | collective-permute-done | bytes 131104 | tf_op jit(solution)/shard_map/ppermute | solution.py:221
  90.4 0.8 shard_map.57.refs_4_
  91.3 0.0 collective-permute-done.4.refs_0_
  91.3 0.0 collective-permute-done.5.refs_1_
  91.3 1.2 %shard_map.58 = bf16[256,4096]{1,0:T(8,128)(2,1)} custom-call(bf16[128,1536]{1,0:T(8,128)(2,1)S(1)} %collective-permute-done.4.refs_0_, bf16[128,1536]{1,0:T(8,128)(2,1)S(1)} %collective-permute-done.5.refs_1_, bf16[128,1536]{1,0:T(8,128)(2,1)S(1)} %collective-permute-done.6.refs_2_, ...), custom_call_target="tpu_custom_call", output_to_operand_aliasing={{}: (4, {})} | custom-call | tf_op jit(solution)/shard_map/pallas_call | solution.py:290
  (5 shorter events, 0.0 us)
Async XLA Ops:
  1.3 28.5 %collective-permute-start.3 = (bf16[128,1536]{1,0:T(8,128)(2,1)S(1)}, bf16[128,1536]{1,0:T(8,128)(2,1)S(1)}, u32[]{:S(2)}, u32[]{:S(2)}) collective-permute-start(bf16[128,1536]{1,0:T(8,128)(2,1)S(1)} %get-tuple-element.22), channel_id=1, source_target_pairs={{0,2},{2,0},{4,6},{6,4},{8,10},{10,8},{12,14},{14,12},{1,3},{3,1},... | collective-permute-start | bytes 1179656 | tf_op jit(solution)/shard_map/ppermute | solution.py:221
  1.4 19.3 %collective-permute-start.2 = (bf16[128,1024]{1,0:T(8,128)(2,1)S(1)}, bf16[128,1024]{1,0:T(8,128)(2,1)S(1)}, u32[]{:S(2)}, u32[]{:S(2)}) collective-permute-start(bf16[128,1024]{1,0:T(8,128)(2,1)S(1)} %get-tuple-element.21), channel_id=1, source_target_pairs={{0,2},{2,0},{4,6},{6,4},{8,10},{10,8},{12,14},{14,12},{1,3},{3,1},... | collective-permute-start | bytes 786440 | tf_op jit(solution)/shard_map/ppermute | solution.py:221
  3.4 8.8 %collective-permute-start.1 = (bf16[128,512]{1,0:T(8,128)(2,1)S(1)}, bf16[128,512]{1,0:T(8,128)(2,1)S(1)}, u32[]{:S(2)}, u32[]{:S(2)}) collective-permute-start(bf16[128,512]{1,0:T(8,128)(2,1)S(1)} %get-tuple-element.20), channel_id=1, source_target_pairs={{0,6},{2,4},{4,10},{6,8},{8,14},{10,12},{12,2},{14,0},{1,7},{3,5},... | collective-permute-start | bytes 393224 | tf_op jit(solution)/shard_map/ppermute | solution.py:221
  5.0 7.8 %collective-permute-start = (bf16[128,512]{1,0:T(8,128)(2,1)S(1)}, bf16[128,512]{1,0:T(8,128)(2,1)S(1)}, u32[]{:S(2)}, u32[]{:S(2)}) collective-permute-start(bf16[128,512]{1,0:T(8,128)(2,1)S(1)} %get-tuple-element.19.refs_3_), channel_id=1, source_target_pairs={{0,4},{2,6},{4,8},{6,10},{8,12},{10,14},{12,0},{14,2},{1,5},{3,7},... | collective-permute-start | bytes 393224 | tf_op jit(solution)/shard_map/ppermute | solution.py:221
  22.8 29.0 %collective-permute-start.8 = (bf16[128,512]{1,0:T(8,128)(2,1)S(1)}, bf16[128,512]{1,0:T(8,128)(2,1)S(1)}, u32[]{:S(2)}, u32[]{:S(2)}) collective-permute-start(bf16[128,512]{1,0:T(8,128)(2,1)S(1)} %get-tuple-element.27), channel_id=1, source_target_pairs={{0,0},{2,8},{4,4},{6,12},{8,10},{10,2},{12,14},{14,6},{1,1},{3,9},... | collective-permute-start | bytes 393224 | tf_op jit(solution)/shard_map/ppermute | solution.py:221
  27.3 24.5 %collective-permute-start.9 = (bf16[128,512]{1,0:T(8,128)(2,1)S(1)}, bf16[128,512]{1,0:T(8,128)(2,1)S(1)}, u32[]{:S(2)}, u32[]{:S(2)}) collective-permute-start(bf16[128,512]{1,0:T(8,128)(2,1)S(1)} %get-tuple-element.28), channel_id=1, source_target_pairs={{0,4},{2,12},{4,0},{6,8},{8,14},{10,6},{12,10},{14,2},{1,5},{3,13}... | collective-permute-start | bytes 393224 | tf_op jit(solution)/shard_map/ppermute | solution.py:221
  33.2 58.1 %collective-permute-start.4 = (bf16[128,1536]{1,0:T(8,128)(2,1)S(1)}, bf16[128,1536]{1,0:T(8,128)(2,1)S(1)}, u32[]{:S(2)}, u32[]{:S(2)}) collective-permute-start(bf16[128,1536]{1,0:T(8,128)(2,1)S(1)} %get-tuple-element.23), channel_id=1, source_target_pairs={{0,0},{2,8},{4,4},{6,12},{8,10},{10,2},{12,14},{14,6},{1,1},{3,9},... | collective-permute-start | bytes 1179656 | tf_op jit(solution)/shard_map/ppermute | solution.py:221
  35.4 55.9 %collective-permute-start.5 = (bf16[128,1536]{1,0:T(8,128)(2,1)S(1)}, bf16[128,1536]{1,0:T(8,128)(2,1)S(1)}, u32[]{:S(2)}, u32[]{:S(2)}) collective-permute-start(bf16[128,1536]{1,0:T(8,128)(2,1)S(1)} %get-tuple-element.24), channel_id=1, source_target_pairs={{0,4},{2,12},{4,0},{6,8},{8,14},{10,6},{12,10},{14,2},{1,5},{3,13}... | collective-permute-start | bytes 1179656 | tf_op jit(solution)/shard_map/ppermute | solution.py:221
  37.9 53.4 %collective-permute-start.6 = (bf16[128,1536]{1,0:T(8,128)(2,1)S(1)}, bf16[128,1536]{1,0:T(8,128)(2,1)S(1)}, u32[]{:S(2)}, u32[]{:S(2)}) collective-permute-start(bf16[128,1536]{1,0:T(8,128)(2,1)S(1)} %get-tuple-element.25), channel_id=1, source_target_pairs={{0,8},{2,0},{4,12},{6,4},{8,2},{10,10},{12,6},{14,14},{1,9},{3,1},... | collective-permute-start | bytes 1179656 | tf_op jit(solution)/shard_map/ppermute | solution.py:221
  51.8 39.5 %collective-permute-start.7 = (bf16[128,1536]{1,0:T(8,128)(2,1)S(1)}, bf16[128,1536]{1,0:T(8,128)(2,1)S(1)}, u32[]{:S(2)}, u32[]{:S(2)}) collective-permute-start(bf16[128,1536]{1,0:T(8,128)(2,1)S(1)} %get-tuple-element.26), channel_id=1, source_target_pairs={{0,12},{2,4},{4,8},{6,0},{8,6},{10,14},{12,2},{14,10},{1,13},{3,5}... | collective-permute-start | bytes 1179656 | tf_op jit(solution)/shard_map/ppermute | solution.py:221
  51.8 31.0 %collective-permute-start.10 = (bf16[128,512]{1,0:T(8,128)(2,1)S(1)}, bf16[128,512]{1,0:T(8,128)(2,1)S(1)}, u32[]{:S(2)}, u32[]{:S(2)}) collective-permute-start(bf16[128,512]{1,0:T(8,128)(2,1)S(1)} %get-tuple-element.29), channel_id=1, source_target_pairs={{0,8},{2,0},{4,12},{6,4},{8,2},{10,10},{12,6},{14,14},{1,9},{3,1},... | collective-permute-start | bytes 393224 | tf_op jit(solution)/shard_map/ppermute | solution.py:221
  82.8 7.7 %collective-permute-start.11 = (bf16[128,512]{1,0:T(8,128)(2,1)S(1)}, bf16[128,512]{1,0:T(8,128)(2,1)S(1)}, u32[]{:S(2)}, u32[]{:S(2)}) collective-permute-start(bf16[128,512]{1,0:T(8,128)(2,1)S(1)} %get-tuple-element.30), channel_id=1, source_target_pairs={{0,12},{2,4},{4,8},{6,0},{8,6},{10,14},{12,2},{14,10},{1,13},{3,5}... | collective-permute-start | bytes 393224 | tf_op jit(solution)/shard_map/ppermute | solution.py:221

commit v2 on v0

--- a/solution.py
+++ b/solution.py
@@ -19,6 +19,7 @@
 exponent_scale = math.log2(math.e) / math.sqrt(HEAD_WIDTH)
 vmem = pl.BlockSpec(memory_space=pltpu.VMEM)
 smem = pl.BlockSpec(memory_space=pltpu.SMEM)
+anywhere = pl.BlockSpec(memory_space=pl.ANY)
 hbm = pl.BlockSpec(memory_space=pltpu.HBM)
 
 
@@ -37,6 +38,35 @@
 
 def kv_first(blk, dev_width):
     return blk * dev_width // (HEAD_WIDTH * HEADS_PER_GROUP) * HEAD_WIDTH
+
+
+def kv_range(chunk):
+    first, heads = chunk
+    return first // HEADS_PER_GROUP, (first + heads - 1) // HEADS_PER_GROUP + 1
+
+
+def new_kv(chunks, index):
+    seen = kv_range(chunks[index - 1])[1] if index else 0
+    return seen, kv_range(chunks[index])[1]
+
+
+def cut_choices(seq_count):
+    if seq_count != 4:
+        return []
+    half = seq_count // 2
+    low, high = range(half), range(half, seq_count)
+    up = [(group, owner) for group in low for owner in high]
+    down = [(group, owner) for group in high for owner in low]
+    return [(u, d) for u in up[:2] for d in down[2:]] + [(u, d) for u in up[2:] for d in down[:2]]
+
+
+def is_empty(plan_ref, pair_room, pair):
+    group, owner = pair
+    empty = jnp.bool_(True)
+    for block in range(plan_ref.shape[0]):
+        slot = plan_ref[block, group]
+        empty = empty & ((slot < owner * pair_room) | (slot >= (owner + 1) * pair_room))
+    return empty
 
 
 def pack_kernel(block_axis, dev_width, kv_width, chunks, query_ref, key_ref, value_ref, *refs):
@@ -46,19 +76,24 @@
     moves = [(query_ref.at[:, lanes(blk * dev_width, dev_width)], own_ref)]
     for shift in range(block_axis):
         to = lax.rem(blk + shift, block_axis)
-        kv = lanes(kv_first(to, dev_width), kv_width)
-        targets = [prior_refs[shift]]
+        base = kv_first(to, dev_width)
+        kv = lanes(base, kv_width)
+        moves.append((key_ref.at[:, kv], prior_refs[shift].at[:, pl.ds(0, kv_width)]))
+        moves.append((value_ref.at[:, kv], prior_refs[shift].at[:, pl.ds(kv_width, kv_width)]))
+        if shift == 0:
+            continue
         for chunk, (first, size) in enumerate(chunks):
-            if shift:
-                out_ref = rest[chunk * (block_axis - 1) + shift - 1]
-                columns = lanes(to * dev_width + first * HEAD_WIDTH, size * HEAD_WIDTH)
-                if chunk == 0:
-                    targets.append(out_ref)
-                    out_ref = out_ref.at[:, pl.ds(2 * kv_width, size * HEAD_WIDTH)]
-                moves.append((query_ref.at[:, columns], out_ref))
-        for target in targets:
-            moves.append((key_ref.at[:, kv], target.at[:, pl.ds(0, kv_width)]))
-            moves.append((value_ref.at[:, kv], target.at[:, pl.ds(kv_width, kv_width)]))
+            out_ref = rest[chunk * (block_axis - 1) + shift - 1]
+            low, high = new_kv(chunks, chunk)
+            span = (high - low) * HEAD_WIDTH
+            if span:
+                kv = lanes(base + low * HEAD_WIDTH, span)
+                moves.append((key_ref.at[:, kv], out_ref.at[:, pl.ds(0, span)]))
+                moves.append((value_ref.at[:, kv], out_ref.at[:, pl.ds(span, span)]))
+            columns = lanes(to * dev_width + first * HEAD_WIDTH, size * HEAD_WIDTH)
+            moves.append(
+                (query_ref.at[:, columns], out_ref.at[:, pl.ds(2 * span, size * HEAD_WIDTH)])
+            )
     copies = [
         pltpu.make_async_copy(source, target, sems.at[index])
         for index, (source, target) in enumerate(moves)
@@ -69,25 +104,33 @@
         copy.wait()
 
 
-def attend_kernel(seq_count, block_axis, pair_room, kv_width, chunk, *refs):
+def attend_kernel(seq_count, block_axis, pair_room, kv_width, chunks, cuts, index, *refs):
     refs = list(refs)
     take = lambda count: [refs.pop(0) for _ in range(count)]
     doc_ref, plan_ref, own_query, own_kv = take(4)
     prior_refs = take(block_axis)
-    home_refs = take(block_axis - 1)
-    query_refs = take(block_axis - 1) if chunk[0] else home_refs
+    home_refs = [take(block_axis - 1) for _ in range(index + 1)]
     message_refs = take(seq_count)
+    if index == 0:
+        (choice_ref,) = take(1)
+        empty = {}
+        for pair in sum(cuts, ()):
+            empty[pair] = is_empty(plan_ref, pair_room, pair)
+        choice = jnp.int32(len(cuts))
+        for number, (up, down) in reversed(list(enumerate(cuts))):
+            choice = jnp.where(empty[up] & empty[down], number, choice)
+        choice_ref[0] = choice
     query_all, key_all, value_all = refs
     group = lax.axis_index("seq")
     blk = lax.axis_index("blk")
     group_len = block_axis * BLOCK
     window = group_len + BLOCK
-    first, heads = chunk
+    first, heads = chunks[index]
     columns = heads * HEAD_WIDTH
-    query_at = 0 if first else 2 * kv_width
-    kv_low = first // HEADS_PER_GROUP
-    kv_high = (first + heads - 1) // HEADS_PER_GROUP + 1
+    kv_low, kv_high = kv_range(chunks[index])
     kv_from, kv_to = kv_low * HEAD_WIDTH, kv_high * HEAD_WIDTH
+    new_low, new_high = new_kv(chunks, index)
+    query_at = 2 * (new_high - new_low) * HEAD_WIDTH
     doc_count = doc_ref.shape[0]
 
     for shift in range(block_axis):
@@ -96,12 +139,20 @@
         near_rows = pl.ds(pl.multiple_of(group_len + origin * BLOCK, BLOCK), BLOCK)
         if shift == 0:
             query = own_query[:, first * HEAD_WIDTH : first * HEAD_WIDTH + columns]
-            home = own_kv
+            key_all[near_rows, :] = own_kv[:, kv_from:kv_to]
+            value_all[near_rows, :] = own_kv[:, kv_width + kv_from : kv_width + kv_to]
         else:
-            query = query_refs[shift - 1][:, query_at : query_at + columns]
-            home = home_refs[shift - 1]
-        key_all[near_rows, :] = home[:, kv_from:kv_to]
-        value_all[near_rows, :] = home[:, kv_width + kv_from : kv_width + kv_to]
+            query = home_refs[index][shift - 1][:, query_at : query_at + columns]
+            for came in range(index + 1):
+                low, high = new_kv(chunks, came)
+                span = (high - low) * HEAD_WIDTH
+                skip = max(kv_low - low, 0) * HEAD_WIDTH
+                if skip >= span:
+                    continue
+                to = slice((low - kv_low) * HEAD_WIDTH + skip, (high - kv_low) * HEAD_WIDTH)
+                home = home_refs[came][shift - 1]
+                key_all[near_rows, to] = home[:, skip:span]
+                value_all[near_rows, to] = home[:, span + skip : 2 * span]
         for head in range(heads):
             query_all[origin, head * BLOCK : (head + 1) * BLOCK, :] = query[
                 :, head * HEAD_WIDTH : (head + 1) * HEAD_WIDTH
@@ -182,12 +233,12 @@
     per_owner = seq_count // block_axis
     rows, width = messages[0].shape
     copies = []
-    for step in range(seq_count):
+    for step, message_ref in enumerate(messages):
         origin = lax.rem(group - step + seq_count, seq_count)
         at_rows = pl.ds(pl.multiple_of(lax.rem(origin, per_owner) * rows, rows), rows)
         at_lanes = lanes(origin // per_owner * dev_width + first * HEAD_WIDTH, width)
         copies.append(
-            pltpu.make_async_copy(messages[step], out_ref.at[at_rows, at_lanes], sems.at[step])
+            pltpu.make_async_copy(message_ref, out_ref.at[at_rows, at_lanes], sems.at[step])
         )
     for copy in copies:
         copy.start()
@@ -226,48 +277,46 @@
     bf16 = lambda *shape: jax.ShapeDtypeStruct(shape, jnp.bfloat16)
     peers = block_axis - 1
     out_shape = [bf16(BLOCK, dev_width)] + [bf16(BLOCK, 2 * kv_width)] * block_axis
-    for first, size in chunks:
-        out_shape += [bf16(BLOCK, size * HEAD_WIDTH + (0 if first else 2 * kv_width))] * peers
+    for index, (first, size) in enumerate(chunks):
+        low, high = new_kv(chunks, index)
+        out_shape += [bf16(BLOCK, (size + 2 * (high - low)) * HEAD_WIDTH)] * peers
+    cuts = cut_choices(seq_count)
+    plan = in_hbm(owner_plan.T)
     own_query, *packed = pl.pallas_call(
         lambda *refs: pack_kernel(block_axis, dev_width, kv_width, chunks, *refs),
         out_shape=out_shape,
         in_specs=[hbm] * 3,
         out_specs=[vmem] * len(out_shape),
         scratch_shapes=[
-            pltpu.SemaphoreType.DMA((1 + 2 * block_axis + peers * (2 + len(chunks)),))
+            pltpu.SemaphoreType.DMA((1 + 2 * block_axis + 3 * peers * len(chunks),))
         ],
         compiler_params=pltpu.CompilerParams(vmem_limit_bytes=8 << 20),
         name="pack",
     )(*map(in_hbm, (queries, rotated_keys, head_value_rows)))
 
     sideways = lambda shift: lambda z, x: (z, (x + shift) % block_axis)
-    onward = lambda shift: lambda z, x: (
-        (z + 1, (x + shift) % block_axis) if z + 1 < seq_count else None
-    )
-    home = [permute(packed[block_axis + s - 1], sideways(s)) for s in range(1, block_axis)]
+    onward = lambda shift: lambda z, x: ((z + 1) % seq_count, (x + shift) % block_axis)
+    home = [
+        [permute(packed[block_axis + c * peers + s - 1], sideways(s)) for s in range(1, block_axis)]
+        for c in range(len(chunks))
+    ]
     prior = [permute(packed[s], onward(s)) for s in range(block_axis)]
-    later = [
-        [permute(packed[block_axis + c * peers + s - 1], sideways(s)) for s in range(1, block_axis)]
-        for c in range(1, len(chunks))
-    ]
-
-    out = None
+
+    results = []
     for index, chunk in enumerate(chunks):
         first, heads = chunk
         width = heads * HEAD_WIDTH
-        kv_span = (
-            (first + heads - 1) // HEADS_PER_GROUP + 1 - first // HEADS_PER_GROUP
-        ) * HEAD_WIDTH
-        inputs = [own_query, packed[0], *prior, *home]
-        if index:
-            inputs += later[index - 1]
+        kv_low, kv_high = kv_range(chunk)
+        kv_span = (kv_high - kv_low) * HEAD_WIDTH
+        choices = [] if index else [jax.ShapeDtypeStruct((1,), jnp.int32)]
+        inputs = [own_query, packed[0], *prior, *sum(home[: index + 1], [])]
         attend = pl.pallas_call(
-            lambda *refs, chunk=chunk: attend_kernel(
-                seq_count, block_axis, pair_room, kv_width, chunk, *refs
+            lambda *refs, index=index: attend_kernel(
+                seq_count, block_axis, pair_room, kv_width, chunks, cuts, index, *refs
             ),
-            out_shape=[bf16(slot_rows, width)] * seq_count,
+            out_shape=[bf16(slot_rows, width)] * seq_count + choices,
             in_specs=[smem, smem] + [vmem] * len(inputs),
-            out_specs=[vmem] * seq_count,
+            out_specs=[vmem] * seq_count + [smem] * len(choices),
             scratch_shapes=[
                 pltpu.VMEM((block_axis, heads * BLOCK, HEAD_WIDTH), jnp.bfloat16),
                 pltpu.VMEM((2 * block_axis * BLOCK, kv_span), jnp.bfloat16),
@@ -280,26 +329,44 @@
             ),
             compiler_params=pltpu.CompilerParams(vmem_limit_bytes=16 << 20),
         )
-        messages = attend(in_hbm(doc_lengths), in_hbm(owner_plan.T), *inputs)
-        arrived = [
-            permute(
-                messages[step],
-                lambda z, x: (owner_of(step, z, x, seq_count, block_axis), z // per_owner),
-            )
-            for step in range(seq_count)
+        messages = attend(in_hbm(doc_lengths), plan, *inputs)
+        if index == 0:
+            messages, (choice,) = messages[:-1], messages[-1:]
+        results.append(messages)
+
+    def deliver(left_out, messages):
+        def target(step, z, x):
+            owner = owner_of(step, z, x, seq_count, block_axis)
+            return None if (z, owner) in left_out else (owner, z // per_owner)
+
+        return [
+            permute(message, lambda z, x: target(step, z, x))
+            for step, message in enumerate(messages)
         ]
-        carried = [] if out is None else [out]
-        out = pl.pallas_call(
-            lambda *refs, first=first: place_kernel(
-                seq_count, block_axis, dev_width, first, *refs
-            ),
+
+    def place(index, arrived, *carried):
+        return pl.pallas_call(
+            lambda *refs: place_kernel(seq_count, block_axis, dev_width, chunks[index][0], *refs),
             out_shape=bf16(per_owner * slot_rows, heads_tp * HEAD_WIDTH),
-            in_specs=[vmem] * seq_count + [hbm] * len(carried),
-            out_specs=hbm,
+            in_specs=[vmem] * seq_count + [anywhere] * len(carried),
+            out_specs=anywhere,
             scratch_shapes=[pltpu.SemaphoreType.DMA((seq_count,))],
             input_output_aliases={seq_count: 0} if carried else {},
             compiler_params=pltpu.CompilerParams(vmem_limit_bytes=8 << 20),
         )(*arrived, *carried)
+
+    last = len(chunks) - 1
+    arrived = [deliver((), results[index]) for index in range(last)]
+    if cuts:
+        branches = [
+            lambda *messages, cut=cut: place(last, deliver(cut, messages))
+            for cut in [*cuts, ()]
+        ]
+        out = lax.switch(choice[0], branches, *results[last])
+    else:
+        out = place(last, deliver((), results[last]))
+    for index in range(last):
+        out = place(index, arrived[index], out)
     return out
 
 

time: 88.9 us -> 81.3 us (0.915)
  the two profiles are of different devices: /device:TPU:2 before, /device:TPU:11 now
where the time goes in v2:
time: 81.3 us; the launch traced here: 81.1 us
  waiting for transfers between devices  53 us (65%)
  starting transfers between devices  18.8 us (23%)
  Pallas kernels  8.45 us (10%)
    ppermute x12, waiting for transfers between devices, permute(): return lax.ppermute(array, ('seq', 'blk'), pairs)  53 us
    ppermute x12, starting transfers between devices, permute(): return lax.ppermute(array, ('seq', 'blk'), pairs)  18.8 us
    pallas_call x2, Pallas kernels, per_device(): messages = attend(in_hbm(doc_lengths), plan, *inputs)  6 us
  transfers between devices with their start and end apart: 12, of which 7 were waited for; matrix products, arithmetic and copies ran while one was open for 0% of the time, Pallas kernels for 8%

profile of v2, /device:TPU:11, one launch (start us, length us, event | category | flops | bytes accessed | tf_op | source)
XLA Modules:
  0.0 81.1 jit_solution(9010640612433061193)
XLA Ops:
  0.0 1.4 %pack.1 = (bf16[128,2048]{1,0:T(8,128)(2,1)S(1)}, bf16[128,512]{1,0:T(8,128)(2,1)S(1)}, bf16[128,512]{1,0:T(8,128)(2,1)S(1)}, bf16[128,768]{1,0:T(8,128)(2,1)S(1)}, bf16[128,1792]{1,0:T(8,128)(2,1)S(1)}) custom-call(bf16[128,4096]{1,0:T(8,128)(2,1)} %refs_0_.3, bf16[128,512]{1,0:T(8,128)(2,1)} %refs_1_.1, bf16[128,512]{1,0:T(8,128)(2,1)} %refs_2_.1), custom_call_target="tpu_custom_call" | custom-call | tf_op jit(solution)/shard_map/pack/pallas_call | solution.py:285
  1.4 0.3 collective-permute-start.43
  1.7 1.2 %collective-permute-start.38 = (bf16[128,768]{1,0:T(8,128)(2,1)S(1)}, bf16[128,768]{1,0:T(8,128)(2,1)S(1)}, u32[]{:S(2)}, u32[]{:S(2)}) collective-permute-start(bf16[128,768]{1,0:T(8,128)(2,1)S(1)} %get-tuple-element.136), channel_id=1, source_target_pairs={{0,2},{2,0},{4,6},{6,4},{8,10},{10,8},{12,14},{14,12},{1,3},{3,1},... | collective-permute-start | bytes 589832 | tf_op jit(solution)/shard_map/ppermute | solution.py:272
  3.0 1.3 %collective-permute-start.37 = (bf16[128,512]{1,0:T(8,128)(2,1)S(1)}, bf16[128,512]{1,0:T(8,128)(2,1)S(1)}, u32[]{:S(2)}, u32[]{:S(2)}) collective-permute-start(bf16[128,512]{1,0:T(8,128)(2,1)S(1)} %get-tuple-element.135), channel_id=1, source_target_pairs={{0,6},{2,4},{4,10},{6,8},{8,14},{10,12},{12,2},{14,0},{1,7},{3,5},... | collective-permute-start | bytes 393224 | tf_op jit(solution)/shard_map/ppermute | solution.py:272
  4.2 1.3 %collective-permute-start.36 = (bf16[128,512]{1,0:T(8,128)(2,1)S(1)}, bf16[128,512]{1,0:T(8,128)(2,1)S(1)}, u32[]{:S(2)}, u32[]{:S(2)}) collective-permute-start(bf16[128,512]{1,0:T(8,128)(2,1)S(1)} %get-tuple-element.134.refs_3_), channel_id=1, source_target_pairs={{0,4},{2,6},{4,8},{6,10},{8,12},{10,14},{12,0},{14,2},{1,5},{3,7},... | collective-permute-start | bytes 393224 | tf_op jit(solution)/shard_map/ppermute | solution.py:272
  5.5 2.3 %collective-permute-done.37.refs_5_ = bf16[128,512]{1,0:T(8,128)(2,1)S(1)} collective-permute-done((bf16[128,512]{1,0:T(8,128)(2,1)S(1)}, bf16[128,512]{1,0:T(8,128)(2,1)S(1)}, u32[]{:S(2)}, u32[]{:S(2)}) %collective-permute-start.37) | collective-permute-done | bytes 131104 | tf_op jit(solution)/shard_map/ppermute | solution.py:272
  7.8 1.9 %collective-permute-done.36.refs_4_ = bf16[128,512]{1,0:T(8,128)(2,1)S(1)} collective-permute-done((bf16[128,512]{1,0:T(8,128)(2,1)S(1)}, bf16[128,512]{1,0:T(8,128)(2,1)S(1)}, u32[]{:S(2)}, u32[]{:S(2)}) %collective-permute-start.36) | collective-permute-done | bytes 131104 | tf_op jit(solution)/shard_map/ppermute | solution.py:272
  9.7 10.3 %collective-permute-done.38.refs_6_ = bf16[128,768]{1,0:T(8,128)(2,1)S(1)} collective-permute-done((bf16[128,768]{1,0:T(8,128)(2,1)S(1)}, bf16[128,768]{1,0:T(8,128)(2,1)S(1)}, u32[]{:S(2)}, u32[]{:S(2)}) %collective-permute-start.38) | collective-permute-done | bytes 196640 | tf_op jit(solution)/shard_map/ppermute | solution.py:272
  19.9 2.7 %shard_map.55 = (bf16[128,512]{1,0:T(8,128)(2,1)S(1)}, bf16[128,512]{1,0:T(8,128)(2,1)S(1)}, bf16[128,512]{1,0:T(8,128)(2,1)S(1)}, bf16[128,512]{1,0:T(8,128)(2,1)S(1)}, s32[1]{0:T(128)}) custom-call(s32[8]{0:T(128)} %refs_0_.5, s32[2,4]{1,0:T(2,128)} %bitcast.2, bf16[128,2048]{1,0:T(8,128)(2,1)S(1)} %get-tuple-element.133.refs_2_, ...), custom_call_target="tpu_custom_call" | custom-call | flops 402653184 | bytes 524288 | tf_op jit(solution)/shard_map/pallas_call | solution.py:332
  22.6 4.2 %collective-permute-start.39 = (bf16[128,512]{1,0:T(8,128)(2,1)S(1)}, bf16[128,512]{1,0:T(8,128)(2,1)S(1)}, u32[]{:S(2)}, u32[]{:S(2)}) collective-permute-start(bf16[128,512]{1,0:T(8,128)(2,1)S(1)} %get-tuple-element.137), channel_id=1, source_target_pairs={{0,0},{2,8},{4,4},{6,12},{8,2},{10,10},{12,6},{14,14},{1,1},{3,9},... | collective-permute-start | bytes 393224 | tf_op jit(solution)/shard_map/ppermute | solution.py:272
  27.4 3.3 %shard_map.56 = (bf16[128,1536]{1,0:T(8,128)(2,1)S(1)}, bf16[128,1536]{1,0:T(8,128)(2,1)S(1)}, bf16[128,1536]{1,0:T(8,128)(2,1)S(1)}, bf16[128,1536]{1,0:T(8,128)(2,1)S(1)}) custom-call(s32[8]{0:T(128)} %refs_0_.5, s32[2,4]{1,0:T(2,128)} %bitcast.3, bf16[128,2048]{1,0:T(8,128)(2,1)S(1)} %get-tuple-element.133.refs_2_, ...), custom_call_target="tpu_custom_call" | custom-call | flops 1207959552 | bytes 1572864 | tf_op jit(solution)/shard_map/pallas_call | solution.py:332
  30.8 28.7 %conditional.1 = (bf16[256,4096]{1,0:T(8,128)(2,1)S(1)}) conditional(s32[]{:T(128)} %bitcast.1, (bf16[128,1536]{1,0:T(8,128)(2,1)S(1)}, bf16[128,1536]{1,0:T(8,128)(2,1)S(1)}, bf16[128,1536]{1,0:T(8,128)(2,1)S(1)}, bf16[128,1536]{1,0:T(8,128)(2,1)S(1)}) %shard_map.56, (bf16[128,1536]{1,0:T(8,128)(2,1)S(1)}, ...), branch_computations={%region_0.0_spmd, %region_1.0_spmd, %region_2.0_spmd, %region_3.0_... | conditional | bytes 6291624 | solution.py:365
  30.8 2.9 %collective-permute-start.20 = (bf16[128,1536]{1,0:T(8,128)(2,1)S(1)}, bf16[128,1536]{1,0:T(8,128)(2,1)S(1)}, u32[]{:S(2)}, u32[]{:S(2)}) collective-permute-start(bf16[128,1536]{1,0:T(8,128)(2,1)S(1)} %get-tuple-element.107), channel_id=1, source_target_pairs={{0,0},{2,8},{4,4},{6,12},{8,2},{10,10},{12,6},{14,14},{1,1},{3,9},... | collective-permute-start | bytes 1179656 | tf_op jit(solution)/shard_map/cond/branch_5_fun/ppermute | solution.py:272
  33.7 1.3 %collective-permute-start.21 = (bf16[128,1536]{1,0:T(8,128)(2,1)S(1)}, bf16[128,1536]{1,0:T(8,128)(2,1)S(1)}, u32[]{:S(2)}, u32[]{:S(2)}) collective-permute-start(bf16[128,1536]{1,0:T(8,128)(2,1)S(1)} %get-tuple-element.108), channel_id=1, source_target_pairs={{0,4},{2,12},{6,0},{10,14},{12,10},{14,2},{1,5},{3,13},{7,1},{11,1... | collective-permute-start | bytes 1179656 | tf_op jit(solution)/shard_map/cond/branch_5_fun/ppermute | solution.py:272
  35.0 0.1 collective-permute-start.22
  35.1 0.7 collective-permute-start.23
  35.8 23.5 %collective-permute-done.20.refs_0_ = bf16[128,1536]{1,0:T(8,128)(2,1)S(1)} collective-permute-done((bf16[128,1536]{1,0:T(8,128)(2,1)S(1)}, bf16[128,1536]{1,0:T(8,128)(2,1)S(1)}, u32[]{:S(2)}, u32[]{:S(2)}) %collective-permute-start.20) | collective-permute-done | bytes 393248 | tf_op jit(solution)/shard_map/cond/branch_5_fun/ppermute | solution.py:272
  59.3 0.2 branch_5_fun.1
  59.5 5.1 %collective-permute-start.40 = (bf16[128,512]{1,0:T(8,128)(2,1)S(1)}, bf16[128,512]{1,0:T(8,128)(2,1)S(1)}, u32[]{:S(2)}, u32[]{:S(2)}) collective-permute-start(bf16[128,512]{1,0:T(8,128)(2,1)S(1)} %get-tuple-element.138), channel_id=1, source_target_pairs={{0,4},{2,12},{4,8},{6,0},{8,6},{10,14},{12,10},{14,2},{1,5},{3,13}... | collective-permute-start | bytes 393224 | tf_op jit(solution)/shard_map/ppermute | solution.py:272
  64.7 0.5 collective-permute-start.42
  65.1 1.5 %collective-permute-done.40.refs_1_ = bf16[128,512]{1,0:T(8,128)(2,1)S(1)} collective-permute-done((bf16[128,512]{1,0:T(8,128)(2,1)S(1)}, bf16[128,512]{1,0:T(8,128)(2,1)S(1)}, u32[]{:S(2)}, u32[]{:S(2)}) %collective-permute-start.40) | collective-permute-done | bytes 131104 | tf_op jit(solution)/shard_map/ppermute | solution.py:272
  66.6 7.2 %collective-permute-done.41.refs_2_ = bf16[128,512]{1,0:T(8,128)(2,1)S(1)} collective-permute-done((bf16[128,512]{1,0:T(8,128)(2,1)S(1)}, bf16[128,512]{1,0:T(8,128)(2,1)S(1)}, u32[]{:S(2)}, u32[]{:S(2)}) %collective-permute-start.41) | collective-permute-done | bytes 131104 | tf_op jit(solution)/shard_map/ppermute | solution.py:272
  73.8 6.4 %collective-permute-done.42.refs_3_ = bf16[128,512]{1,0:T(8,128)(2,1)S(1)} collective-permute-done((bf16[128,512]{1,0:T(8,128)(2,1)S(1)}, bf16[128,512]{1,0:T(8,128)(2,1)S(1)}, u32[]{:S(2)}, u32[]{:S(2)}) %collective-permute-start.42) | collective-permute-done | bytes 131104 | tf_op jit(solution)/shard_map/ppermute | solution.py:272
  80.3 0.8 %shard_map.57 = bf16[256,4096]{1,0:T(8,128)(2,1)} custom-call(bf16[128,512]{1,0:T(8,128)(2,1)S(1)} %collective-permute-done.39.refs_0_, bf16[128,512]{1,0:T(8,128)(2,1)S(1)} %collective-permute-done.40.refs_1_, bf16[128,512]{1,0:T(8,128)(2,1)S(1)} %collective-permute-done.41.refs_2_, ...), custom_call_target="tpu_custom_call", output_to_operand_aliasing={{}: (4, {})} | custom-call | tf_op jit(solution)/shard_map/pallas_call | solution.py:348
  (8 shorter events, 0.0 us)
Async XLA Ops:
  1.4 26.0 %collective-permute-start.43 = (bf16[128,1792]{1,0:T(8,128)(2,1)S(1)}, bf16[128,1792]{1,0:T(8,128)(2,1)S(1)}, u32[]{:S(2)}, u32[]{:S(2)}) collective-permute-start(bf16[128,1792]{1,0:T(8,128)(2,1)S(1)} %get-tuple-element.142), channel_id=1, source_target_pairs={{0,2},{2,0},{4,6},{6,4},{8,10},{10,8},{12,14},{14,12},{1,3},{3,1},... | collective-permute-start | bytes 1376264 | tf_op jit(solution)/shard_map/ppermute | solution.py:272
  1.7 18.2 %collective-permute-start.38 = (bf16[128,768]{1,0:T(8,128)(2,1)S(1)}, bf16[128,768]{1,0:T(8,128)(2,1)S(1)}, u32[]{:S(2)}, u32[]{:S(2)}) collective-permute-start(bf16[128,768]{1,0:T(8,128)(2,1)S(1)} %get-tuple-element.136), channel_id=1, source_target_pairs={{0,2},{2,0},{4,6},{6,4},{8,10},{10,8},{12,14},{14,12},{1,3},{3,1},... | collective-permute-start | bytes 589832 | tf_op jit(solution)/shard_map/ppermute | solution.py:272
  3.0 4.8 %collective-permute-start.37 = (bf16[128,512]{1,0:T(8,128)(2,1)S(1)}, bf16[128,512]{1,0:T(8,128)(2,1)S(1)}, u32[]{:S(2)}, u32[]{:S(2)}) collective-permute-start(bf16[128,512]{1,0:T(8,128)(2,1)S(1)} %get-tuple-element.135), channel_id=1, source_target_pairs={{0,6},{2,4},{4,10},{6,8},{8,14},{10,12},{12,2},{14,0},{1,7},{3,5},... | collective-permute-start | bytes 393224 | tf_op jit(solution)/shard_map/ppermute | solution.py:272
  4.2 5.4 %collective-permute-start.36 = (bf16[128,512]{1,0:T(8,128)(2,1)S(1)}, bf16[128,512]{1,0:T(8,128)(2,1)S(1)}, u32[]{:S(2)}, u32[]{:S(2)}) collective-permute-start(bf16[128,512]{1,0:T(8,128)(2,1)S(1)} %get-tuple-element.134.refs_3_), channel_id=1, source_target_pairs={{0,4},{2,6},{4,8},{6,10},{8,12},{10,14},{12,0},{14,2},{1,5},{3,7},... | collective-permute-start | bytes 393224 | tf_op jit(solution)/shard_map/ppermute | solution.py:272
  22.6 42.5 %collective-permute-start.39 = (bf16[128,512]{1,0:T(8,128)(2,1)S(1)}, bf16[128,512]{1,0:T(8,128)(2,1)S(1)}, u32[]{:S(2)}, u32[]{:S(2)}) collective-permute-start(bf16[128,512]{1,0:T(8,128)(2,1)S(1)} %get-tuple-element.137), channel_id=1, source_target_pairs={{0,0},{2,8},{4,4},{6,12},{8,2},{10,10},{12,6},{14,14},{1,1},{3,9},... | collective-permute-start | bytes 393224 | tf_op jit(solution)/shard_map/ppermute | solution.py:272
  30.8 28.4 %collective-permute-start.20 = (bf16[128,1536]{1,0:T(8,128)(2,1)S(1)}, bf16[128,1536]{1,0:T(8,128)(2,1)S(1)}, u32[]{:S(2)}, u32[]{:S(2)}) collective-permute-start(bf16[128,1536]{1,0:T(8,128)(2,1)S(1)} %get-tuple-element.107), channel_id=1, source_target_pairs={{0,0},{2,8},{4,4},{6,12},{8,2},{10,10},{12,6},{14,14},{1,1},{3,9},... | collective-permute-start | bytes 1179656 | tf_op jit(solution)/shard_map/cond/branch_5_fun/ppermute | solution.py:272
  33.7 25.6 %collective-permute-start.21 = (bf16[128,1536]{1,0:T(8,128)(2,1)S(1)}, bf16[128,1536]{1,0:T(8,128)(2,1)S(1)}, u32[]{:S(2)}, u32[]{:S(2)}) collective-permute-start(bf16[128,1536]{1,0:T(8,128)(2,1)S(1)} %get-tuple-element.108), channel_id=1, source_target_pairs={{0,4},{2,12},{6,0},{10,14},{12,10},{14,2},{1,5},{3,13},{7,1},{11,1... | collective-permute-start | bytes 1179656 | tf_op jit(solution)/shard_map/cond/branch_5_fun/ppermute | solution.py:272
  35.0 24.2 %collective-permute-start.22 = (bf16[128,1536]{1,0:T(8,128)(2,1)S(1)}, bf16[128,1536]{1,0:T(8,128)(2,1)S(1)}, u32[]{:S(2)}, u32[]{:S(2)}) collective-permute-start(bf16[128,1536]{1,0:T(8,128)(2,1)S(1)} %get-tuple-element.109), channel_id=1, source_target_pairs={{0,8},{2,0},{4,12},{6,4},{8,10},{10,2},{12,14},{14,6},{1,9},{3,1},... | collective-permute-start | bytes 1179656 | tf_op jit(solution)/shard_map/cond/branch_5_fun/ppermute | solution.py:272
  35.1 24.2 %collective-permute-start.23 = (bf16[128,1536]{1,0:T(8,128)(2,1)S(1)}, bf16[128,1536]{1,0:T(8,128)(2,1)S(1)}, u32[]{:S(2)}, u32[]{:S(2)}) collective-permute-start(bf16[128,1536]{1,0:T(8,128)(2,1)S(1)} %get-tuple-element.110), channel_id=1, source_target_pairs={{0,12},{2,4},{4,0},{8,14},{12,2},{14,10},{1,13},{3,5},{5,1},{9,15}... | collective-permute-start | bytes 1179656 | tf_op jit(solution)/shard_map/cond/branch_5_fun/ppermute | solution.py:272
  59.5 20.7 %copy-start = (bf16[256,4096]{1,0:T(8,128)(2,1)}, bf16[256,4096]{1,0:T(8,128)(2,1)S(1)}, u32[]{:S(2)}) copy-start(bf16[256,4096]{1,0:T(8,128)(2,1)S(1)} %get-tuple-element.143.refs_4_) | copy-start | bytes 6291460
  59.5 7.1 %collective-permute-start.40 = (bf16[128,512]{1,0:T(8,128)(2,1)S(1)}, bf16[128,512]{1,0:T(8,128)(2,1)S(1)}, u32[]{:S(2)}, u32[]{:S(2)}) collective-permute-start(bf16[128,512]{1,0:T(8,128)(2,1)S(1)} %get-tuple-element.138), channel_id=1, source_target_pairs={{0,4},{2,12},{4,8},{6,0},{8,6},{10,14},{12,10},{14,2},{1,5},{3,13}... | collective-permute-start | bytes 393224 | tf_op jit(solution)/shard_map/ppermute | solution.py:272
  64.7 9.2 %collective-permute-start.41 = (bf16[128,512]{1,0:T(8,128)(2,1)S(1)}, bf16[128,512]{1,0:T(8,128)(2,1)S(1)}, u32[]{:S(2)}, u32[]{:S(2)}) collective-permute-start(bf16[128,512]{1,0:T(8,128)(2,1)S(1)} %get-tuple-element.139), channel_id=1, source_target_pairs={{0,8},{2,0},{4,12},{6,4},{8,10},{10,2},{12,14},{14,6},{1,9},{3,1},... | collective-permute-start | bytes 393224 | tf_op jit(solution)/shard_map/ppermute | solution.py:272
  64.7 15.6 %collective-permute-start.42 = (bf16[128,512]{1,0:T(8,128)(2,1)S(1)}, bf16[128,512]{1,0:T(8,128)(2,1)S(1)}, u32[]{:S(2)}, u32[]{:S(2)}) collective-permute-start(bf16[128,512]{1,0:T(8,128)(2,1)S(1)} %get-tuple-element.140), channel_id=1, source_target_pairs={{0,12},{2,4},{4,0},{6,8},{8,14},{10,6},{12,2},{14,10},{1,13},{3,5}... | collective-permute-start | bytes 393224 | tf_op jit(solution)/shard_map/ppermute | solution.py:272

commit v3 on v2

v3 whole, which is shorter than its diff:
```python
import math

import jax
import jax.numpy as jnp
from jax import lax
from jax.experimental import pallas as pl
from jax.experimental.pallas import tpu as pltpu
from jax.sharding import PartitionSpec as P


QUERY_HEADS = 64
KEY_HEADS = 8
HEAD_WIDTH = 128
BLOCK = 128
HEADS_PER_GROUP = QUERY_HEADS // KEY_HEADS


masked_score = -1e30
exponent_scale = math.log2(math.e) / math.sqrt(HEAD_WIDTH)
vmem = pl.BlockSpec(memory_space=pltpu.VMEM)
smem = pl.BlockSpec(memory_space=pltpu.SMEM)
anywhere = pl.BlockSpec(memory_space=pl.ANY)
hbm = pl.BlockSpec(memory_space=pltpu.HBM)


def owner_of(step, group, blk, seq_count, block_axis):
    per_owner = seq_count // block_axis
    return (step + blk * per_owner + group % per_owner) % seq_count


def in_hbm(array):
    return pltpu.with_memory_space_constraint(array, pltpu.HBM)


def lanes(first, size):
    return pl.ds(pl.multiple_of(first, HEAD_WIDTH), size)


def kv_first(blk, dev_width):
    return blk * dev_width // (HEAD_WIDTH * HEADS_PER_GROUP) * HEAD_WIDTH


def kv_range(chunk):
    first, heads = chunk
    return first // HEADS_PER_GROUP, (first + heads - 1) // HEADS_PER_GROUP + 1


def new_kv(chunks, index):
    seen = kv_range(chunks[index - 1])[1] if index else 0
    return seen, kv_range(chunks[index])[1]


def cut_choices(seq_count):
    if seq_count != 4:
        return []
    half = seq_count // 2
    low, high = range(half), range(half, seq_count)
    up = [(group, owner) for group in low for owner in high]
    down = [(group, owner) for group in high for owner in low]
    order = ((0, 1), (0, 2), (0, 3), (1, 2), (1, 3), (2, 0), (2, 3), (3, 0), (3, 1))
    return [(up[u], down[d]) for u, d in order]


def is_empty(plan_ref, pair_room, pair):
    group, owner = pair
    empty = jnp.bool_(True)
    for block in range(plan_ref.shape[0]):
        slot = plan_ref[block, group]
        empty = empty & ((slot < owner * pair_room) | (slot >= (owner + 1) * pair_room))
    return empty


def pack_kernel(block_axis, dev_width, kv_width, chunks, query_ref, key_ref, value_ref, *refs):
    refs = list(refs)
    blk = lax.axis_index("blk")
    sems = refs.pop()
    moves = []

    def move_kv(target_ref, to, low, high):
        span = (high - low) * HEAD_WIDTH
        kv = lanes(kv_first(to, dev_width) + low * HEAD_WIDTH, span)
        for index, source_ref in enumerate((key_ref, value_ref)):
            moves.append((source_ref.at[:, kv], target_ref.at[:, pl.ds(index * span, span)]))

    def move_query(target_ref, to, first, size, at):
        columns = lanes(to * dev_width + first * HEAD_WIDTH, size * HEAD_WIDTH)
        target = target_ref.at[:, pl.ds(at, size * HEAD_WIDTH)]
        moves.append((query_ref.at[:, columns], target))

    move_query(refs.pop(0), blk, 0, dev_width // HEAD_WIDTH, 0)
    move_kv(refs.pop(0), blk, 0, kv_width // HEAD_WIDTH)
    for index, (first, size) in enumerate(chunks):
        low, high = new_kv(chunks, index)
        for shift in range(1, block_axis):
            to = lax.rem(blk + shift, block_axis)
            home_ref = refs.pop(0)
            if high > low:
                move_kv(home_ref, to, low, high)
                move_kv(refs.pop(0), to, low, high)
            move_query(home_ref, to, first, size, 2 * (high - low) * HEAD_WIDTH)
    copies = [
        pltpu.make_async_copy(source, target, sems.at[index])
        for index, (source, target) in enumerate(moves)
    ]
    for copy in copies:
        copy.start()
    for copy in copies:
        copy.wait()


def prepare_kernel(block_axis, pair_room, cuts, doc_ref, plan_ref, start_ref, choice_ref):
    group = lax.axis_index("seq")
    first_row = group * block_axis * BLOCK
    row_pos = first_row + lax.broadcasted_iota(jnp.int32, start_ref.shape, 0)

    def reach(index, carried):
        end, start = carried
        end = end + doc_ref[index]
        return end, jnp.where(row_pos >= end, end, start)

    _, start = lax.fori_loop(
        0, doc_ref.shape[0], reach, (jnp.int32(0), jnp.zeros(start_ref.shape, jnp.int32))
    )
    start_ref[...] = start
    empty = {}
    for pair in sum(cuts, ()):
        if pair not in empty:
            empty[pair] = is_empty(plan_ref, pair_room, pair)
    choice = jnp.int32(len(cuts))
    for number, (up, down) in reversed(list(enumerate(cuts))):
        choice = jnp.where(empty[up] & empty[down], number, choice)
    choice_ref[0] = choice


def attend_kernel(seq_count, block_axis, pair_room, kv_width, chunks, index, *refs):
    refs = list(refs)
    take = lambda count: [refs.pop(0) for _ in range(count)]
    plan_ref, start_ref, own_query, own_kv, straight = take(5)
    home_refs, cross_refs = [], []
    for came in range(index + 1):
        low, high = new_kv(chunks, came)
        home_refs.append(take(block_axis - 1))
        cross_refs.append(take(block_axis - 1 if high > low else 0))
    message_refs = take(seq_count)
    query_all, key_all, value_all, result = refs
    group = lax.axis_index("seq")
    blk = lax.axis_index("blk")
    group_len = block_axis * BLOCK
    window = group_len + BLOCK
    first, heads = chunks[index]
    columns = heads * HEAD_WIDTH
    kv_low, kv_high = kv_range(chunks[index])
    kv_from, kv_to = kv_low * HEAD_WIDTH, kv_high * HEAD_WIDTH
    new_low, new_high = new_kv(chunks, index)
    query_at = 2 * (new_high - new_low) * HEAD_WIDTH

    for shift in range(block_axis):
        origin = lax.rem(blk - shift + block_axis, block_axis)
        rows = pl.ds(pl.multiple_of(origin * BLOCK, BLOCK), BLOCK)
        near_rows = pl.ds(pl.multiple_of(group_len + origin * BLOCK, BLOCK), BLOCK)
        if shift == 0:
            query = own_query[:, first * HEAD_WIDTH : first * HEAD_WIDTH + columns]
            for to_rows, source in ((near_rows, own_kv), (rows, straight)):
                key_all[to_rows, :] = source[:, kv_from:kv_to]
                value_all[to_rows, :] = source[:, kv_width + kv_from : kv_width + kv_to]
        else:
            query = home_refs[index][shift - 1][:, query_at : query_at + columns]
            for came in range(index + 1):
                low, high = new_kv(chunks, came)
                span = (high - low) * HEAD_WIDTH
                skip = max(kv_low - low, 0) * HEAD_WIDTH
                if skip >= span:
                    continue
                to = slice((low - kv_low) * HEAD_WIDTH + skip, (high - kv_low) * HEAD_WIDTH)
                for to_rows, sources in ((near_rows, home_refs), (rows, cross_refs)):
                    source = sources[came][shift - 1]
                    key_all[to_rows, to] = source[:, skip:span]
                    value_all[to_rows, to] = source[:, span + skip : 2 * span]
        for head in range(heads):
            query_all[origin, head * BLOCK : (head + 1) * BLOCK, :] = query[
                :, head * HEAD_WIDTH : (head + 1) * HEAD_WIDTH
            ]

    def attend(block, carried):
        first_row = group * group_len + block * BLOCK
        query_pos = first_row + lax.broadcasted_iota(jnp.int32, (BLOCK, window), 0)
        key_pos = first_row - group_len + lax.broadcasted_iota(jnp.int32, (BLOCK, window), 1)
        query_rows = pl.ds(pl.multiple_of(block * BLOCK, BLOCK), BLOCK)
        key_rows = pl.ds(pl.multiple_of(block * BLOCK, BLOCK), window)
        start = jnp.concatenate([start_ref[query_rows, :]] * (window // HEAD_WIDTH), axis=1)
        allowed = (key_pos >= start) & (key_pos <= query_pos)
        for kv in range(kv_low, kv_high):
            low = max(first, kv * HEADS_PER_GROUP) - first
            high = min(first + heads, (kv + 1) * HEADS_PER_GROUP) - first
            kv_at = slice((kv - kv_low) * HEAD_WIDTH, (kv - kv_low + 1) * HEAD_WIDTH)
            scores = lax.dot_general(
                query_all[block, low * BLOCK : high * BLOCK, :],
                key_all[key_rows, kv_at],
                (((1,), (1,)), ((), ())),
                preferred_element_type=jnp.float32,
            )
            weights, totals = [], []
            for head in range(high - low):
                score = scores[head * BLOCK : (head + 1) * BLOCK]
                score = jnp.where(allowed, score, masked_score)
                top = jnp.max(score, axis=1, keepdims=True)
                weight = jnp.exp2((score - top) * exponent_scale)
                totals.append(jnp.sum(weight, axis=1, keepdims=True))
                weights.append(weight.astype(jnp.bfloat16))
            mixed = jnp.dot(
                jnp.concatenate(weights, axis=0),
                value_all[key_rows, kv_at],
                preferred_element_type=jnp.float32,
            )
            for head in range(high - low):
                at = slice((low + head) * HEAD_WIDTH, (low + head + 1) * HEAD_WIDTH)
                result[block, :, at] = (
                    mixed[head * BLOCK : (head + 1) * BLOCK] / totals[head]
                ).astype(jnp.bfloat16)
        return carried

    lax.fori_loop(0, block_axis, attend, 0)

    for step in range(seq_count):
        owner = owner_of(step, group, blk, seq_count, block_axis)
        for pair in range(pair_room):
            chosen = jnp.int32(-1)
            for block in range(plan_ref.shape[0]):
                chosen = jnp.where(
                    plan_ref[block, group] == owner * pair_room + pair, block, chosen
                )
            out_rows = slice(pair * BLOCK, (pair + 1) * BLOCK)

            @pl.when(chosen >= 0)
            def _():
                message_refs[step][out_rows, :] = result[chosen]

            @pl.when(chosen < 0)
            def _():
                message_refs[step][out_rows, :] = jnp.zeros((BLOCK, columns), jnp.bfloat16)


def place_kernel(seq_count, block_axis, places, *refs):
    *sources, out_ref, sems = refs
    group = lax.axis_index("seq")
    per_owner = seq_count // block_axis
    moves = []
    for first, stride in places:
        if len(sources) == 1:
            (whole,) = sources
            width = whole.shape[1] // block_axis
            for blk in range(block_axis):
                target = out_ref.at[:, pl.ds(first + blk * stride, width)]
                moves.append((whole.at[:, pl.ds(blk * width, width)], target))
            break
        for step in range(seq_count):
            message_ref = sources.pop(0)
            rows, width = message_ref.shape
            origin = lax.rem(group - step + seq_count, seq_count)
            at_rows = pl.ds(pl.multiple_of(lax.rem(origin, per_owner) * rows, rows), rows)
            at_lanes = lanes(first + origin // per_owner * stride, width)
            moves.append((message_ref, out_ref.at[at_rows, at_lanes]))
    copies = [
        pltpu.make_async_copy(source, target, sems.at[index])
        for index, (source, target) in enumerate(moves)
    ]
    for copy in copies:
        copy.start()
    for copy in copies:
        copy.wait()


def per_device(queries, rotated_keys, head_value_rows, doc_lengths, owner_plan):
    block_axis = lax.axis_size("blk")
    seq_count = lax.axis_size("seq")
    local_tokens = queries.shape[0]
    group_blocks = local_tokens * block_axis // BLOCK
    heads_tp = queries.shape[1] // HEAD_WIDTH
    heads_dev = heads_tp // block_axis
    groups_kv = max(1, heads_dev // HEADS_PER_GROUP)
    dev_width = heads_dev * HEAD_WIDTH
    kv_width = groups_kv * HEAD_WIDTH
    pair_room = -(-2 * group_blocks // seq_count)
    per_owner = seq_count // block_axis
    slot_rows = pair_room * BLOCK
    window = (block_axis + 1) * BLOCK
    assert local_tokens == BLOCK and seq_count % block_axis == 0

    def permute(array, target):
        pairs = []
        for z in range(seq_count):
            for x in range(block_axis):
                to = target(z, x)
                if to is not None:
                    pairs.append((z * block_axis + x, to[0] * block_axis + to[1]))
        return lax.ppermute(array, ("seq", "blk"), pairs)

    early = heads_dev * 5 // 16
    head_counts = [early, heads_dev - early]
    chunks = [(sum(head_counts[:i]), count) for i, count in enumerate(head_counts)]
    cuts = cut_choices(seq_count)
    plan = in_hbm(owner_plan.T)
    peers = block_axis - 1

    bf16 = lambda *shape: jax.ShapeDtypeStruct(shape, jnp.bfloat16)
    entries = [("own_query", dev_width), ("own_kv", 2 * kv_width)]
    for index, (first, size) in enumerate(chunks):
        low, high = new_kv(chunks, index)
        span = 2 * (high - low) * HEAD_WIDTH
        for _ in range(1, block_axis):
            entries.append((f"home_{index}", span + size * HEAD_WIDTH))
            if span:
                entries.append((f"cross_{index}", span))
    packed = pl.pallas_call(
        lambda *refs: pack_kernel(block_axis, dev_width, kv_width, chunks, *refs),
        out_shape=[bf16(BLOCK, width) for _, width in entries],
        in_specs=[hbm] * 3,
        out_specs=[vmem] * len(entries),
        scratch_shapes=[pltpu.SemaphoreType.DMA((3 + 5 * peers * len(chunks),))],
        compiler_params=pltpu.CompilerParams(vmem_limit_bytes=8 << 20),
        name="pack",
    )(*map(in_hbm, (queries, rotated_keys, head_value_rows)))
    named = lambda name: [array for (entry, _), array in zip(entries, packed) if entry == name]
    (own_query,), (own_kv,) = named("own_query"), named("own_kv")

    prepare = pl.pallas_call(
        lambda *refs: prepare_kernel(block_axis, pair_room, cuts, *refs),
        out_shape=[
            jax.ShapeDtypeStruct((block_axis * BLOCK, HEAD_WIDTH), jnp.int32),
            jax.ShapeDtypeStruct((1,), jnp.int32),
        ],
        in_specs=[smem, smem],
        out_specs=[vmem, smem],
        compiler_params=pltpu.CompilerParams(vmem_limit_bytes=8 << 20),
        name="prepare",
    )
    start, choice = prepare(in_hbm(doc_lengths), plan)

    def exchange(index):
        home = [
            permute(array, lambda z, x: (z, (x + shift) % block_axis))
            for shift, array in enumerate(named(f"home_{index}"), 1)
        ]
        return home

    def onward(array, shift):
        return permute(array, lambda z, x: ((z + 1) % seq_count, (x + shift) % block_axis))

    straight = onward(own_kv, 0)
    cross = [
        [onward(array, shift) for shift, array in enumerate(named(f"cross_{index}"), 1)]
        for index in range(len(chunks))
    ]

    def attend(index, homes):
        heads = chunks[index][1]
        width = heads * HEAD_WIDTH
        kv_low, kv_high = kv_range(chunks[index])
        kv_span = (kv_high - kv_low) * HEAD_WIDTH
        inputs = [start, own_query, own_kv, straight]
        for home, crossed in zip(homes, cross):
            inputs += [*home, *crossed]
        return pl.pallas_call(
            lambda *refs: attend_kernel(
                seq_count, block_axis, pair_room, kv_width, chunks, index, *refs
            ),
            out_shape=[bf16(slot_rows, width)] * seq_count,
            in_specs=[smem] + [vmem] * len(inputs),
            out_specs=[vmem] * seq_count,
            scratch_shapes=[
                pltpu.VMEM((block_axis, heads * BLOCK, HEAD_WIDTH), jnp.bfloat16),
                pltpu.VMEM((2 * block_axis * BLOCK, kv_span), jnp.bfloat16),
                pltpu.VMEM((2 * block_axis * BLOCK, kv_span), jnp.bfloat16),
                pltpu.VMEM((block_axis, BLOCK, width), jnp.bfloat16),
            ],
            cost_estimate=pl.CostEstimate(
                flops=8 * group_blocks * BLOCK * window * width,
                bytes_accessed=2 * seq_count * slot_rows * width,
                transcendentals=group_blocks * BLOCK * window * heads,
            ),
            compiler_params=pltpu.CompilerParams(vmem_limit_bytes=16 << 20),
        )(plan, *inputs)

    def deliver(left_out, messages):
        def target(step, z, x):
            owner = owner_of(step, z, x, seq_count, block_axis)
            return None if (z, owner) in left_out else (owner, z // per_owner)

        return [
            permute(message, lambda z, x: target(step, z, x))
            for step, message in enumerate(messages)
        ]

    homes = [exchange(index) for index in range(len(chunks))]
    results = [attend(index, homes[: index + 1]) for index in range(len(chunks))]
    last = len(chunks) - 1
    arrived = [deliver((), results[index]) for index in range(last)]
    last_width = chunks[last][1] * HEAD_WIDTH
    rows = per_owner * slot_rows

    def gather(left_out, messages):
        return pl.pallas_call(
            lambda *refs: place_kernel(seq_count, block_axis, [(0, last_width)], *refs),
            out_shape=bf16(rows, block_axis * last_width),
            in_specs=[vmem] * seq_count,
            out_specs=anywhere,
            scratch_shapes=[pltpu.SemaphoreType.DMA((seq_count,))],
            compiler_params=pltpu.CompilerParams(vmem_limit_bytes=8 << 20),
            name="gather",
        )(*deliver(left_out, messages))

    if cuts:
        branches = [lambda *messages, cut=cut: gather(cut, messages) for cut in [*cuts, ()]]
        gathered = lax.switch(choice[0], branches, *results[last])
    else:
        gathered = gather((), results[last])
    places = [(first * HEAD_WIDTH, dev_width) for first, _ in chunks]
    return pl.pallas_call(
        lambda *refs: place_kernel(seq_count, block_axis, places, *refs),
        out_shape=bf16(rows, heads_tp * HEAD_WIDTH),
        in_specs=[vmem] * (seq_count * last + 1),
        out_specs=hbm,
        scratch_shapes=[pltpu.SemaphoreType.DMA((seq_count * last + block_axis,))],
        compiler_params=pltpu.CompilerParams(vmem_limit_bytes=8 << 20),
        name="place",
    )(*sum(arrived, []), gathered)


def solution(mesh):
    in_specs = (
        P(("groups", "seq", "blk"), "tp"),
        P(("groups", "seq", "blk"), "tp"),
        P(("groups", "seq", "blk"), "tp"),
        P("groups"),
        P("groups", None),
    )
    out_specs = P(("groups", "seq", "blk"), "tp")

    return jax.shard_map(
        per_device, mesh=mesh, in_specs=in_specs, out_specs=out_specs, check_vma=False
    )
```

time: 81.3 us -> 82.4 us (1.014)
  starting transfers between devices: 18.8 us -> 30.2 us
  waiting for transfers between devices: 53 us -> 41.6 us
  Pallas kernels: 8.45 us -> 9.56 us
    ppermute x12 -> x13, waiting for transfers between devices: 53 us -> 41.6 us  [permute(): return lax.ppermute(array, ('seq', 'blk'), pairs)]
    ppermute x12 -> x13, starting transfers between devices: 18.8 us -> 30.2 us  [permute(): return lax.ppermute(array, ('seq', 'blk'), pairs)]
    pallas_call x4 -> x5, Pallas kernels: 7.03 us -> 8.11 us  [the longest x2 5.16 us: attend(): pl.pallas_call(lambda *refs: attend_kernel(seq_count, block_axis, pair_ro...]
  transfers between devices with their start and end apart: 12 -> 13, of which waited for: 7 -> 9; matrix products, arithmetic and copies ran while one was open for 0% -> 0% of each run, Pallas kernels for 8% -> 8%
where the time goes in v3:
time: 82.4 us; the launch traced here: 82.1 us
  waiting for transfers between devices  41.6 us (50%)
  starting transfers between devices  30.2 us (37%)
  Pallas kernels  9.56 us (12%)
    ppermute x13, waiting for transfers between devices, permute(): return lax.ppermute(array, ('seq', 'blk'), pairs)  41.6 us
    ppermute x13, starting transfers between devices, permute(): return lax.ppermute(array, ('seq', 'blk'), pairs)  30.2 us
    pallas_call x2, Pallas kernels, attend(): pl.pallas_call(lambda *refs: attend_kernel(seq_count, block_axis, pair_ro...  5.16 us
  transfers between devices with their start and end apart: 13, of which 9 were waited for; matrix products, arithmetic and copies ran while one was open for 0% of the time, Pallas kernels for 8%

profile of v3, /device:TPU:11, one launch (start us, length us, event | category | flops | bytes accessed | tf_op | source)
XLA Modules:
  0.0 82.1 jit_solution(9874477527292543622)
XLA Ops:
  0.0 1.5 %pack.1 = (bf16[128,2048]{1,0:T(8,128)(2,1)S(1)}, bf16[128,512]{1,0:T(8,128)(2,1)S(1)}, bf16[128,896]{1,0:T(8,128)(2,1)S(1)}, bf16[128,256]{1,0:T(8,128)(2,1)S(1...) custom-call(bf16[128,4096]{1,0:T(8,128)(2,1)} %refs_0_.3, bf16[128,512]{1,0:T(8,128)(2,1)} %refs_1_.1, ...), custom_call_target="tpu_custom_call" | custom-call | tf_op jit(solution)/shard_map/pack/pallas_call | solution.py:314
  1.8 1.2 %collective-permute-start.41 = (bf16[128,896]{1,0:T(8,128)(2,1)S(1)}, bf16[128,896]{1,0:T(8,128)(2,1)S(1)}, u32[]{:S(2)}, u32[]{:S(2)}) collective-permute-start(bf16[128,896]{1,0:T(8,128)(2,1)S(1)} %get-tuple-element.151), channel_id=1, source_target_pairs={{0,2},{2,0},{4,6},{6,4},{8,10},{10,8},{12,14},{14,12},{1,3},{3,1},... | collective-permute-start | bytes 688136 | tf_op jit(solution)/shard_map/ppermute | solution.py:296
  3.0 1.3 %collective-permute-start.40 = (bf16[128,512]{1,0:T(8,128)(2,1)S(1)}, bf16[128,512]{1,0:T(8,128)(2,1)S(1)}, u32[]{:S(2)}, u32[]{:S(2)}) collective-permute-start(bf16[128,512]{1,0:T(8,128)(2,1)S(1)} %get-tuple-element.150.refs_3_), channel_id=1, source_target_pairs={{0,4},{2,6},{4,8},{6,10},{8,12},{10,14},{12,0},{14,2},{1,5},{3,7},... | collective-permute-start | bytes 393224 | tf_op jit(solution)/shard_map/ppermute | solution.py:296
  4.3 1.3 %collective-permute-start.42 = (bf16[128,256]{1,0:T(8,128)(2,1)S(1)}, bf16[128,256]{1,0:T(8,128)(2,1)S(1)}, u32[]{:S(2)}, u32[]{:S(2)}) collective-permute-start(bf16[128,256]{1,0:T(8,128)(2,1)S(1)} %get-tuple-element.152), channel_id=1, source_target_pairs={{0,6},{2,4},{4,10},{6,8},{8,14},{10,12},{12,2},{14,0},{1,7},{3,5},... | collective-permute-start | bytes 196616 | tf_op jit(solution)/shard_map/ppermute | solution.py:296
  5.6 0.9 %collective-permute-start.48 = (bf16[128,256]{1,0:T(8,128)(2,1)S(1)}, bf16[128,256]{1,0:T(8,128)(2,1)S(1)}, u32[]{:S(2)}, u32[]{:S(2)}) collective-permute-start(bf16[128,256]{1,0:T(8,128)(2,1)S(1)} %get-tuple-element.159), channel_id=1, source_target_pairs={{0,6},{2,4},{4,10},{6,8},{8,14},{10,12},{12,2},{14,0},{1,7},{3,5},... | collective-permute-start | bytes 196616 | tf_op jit(solution)/shard_map/ppermute | solution.py:296
  6.5 1.4 %prepare.1 = (s32[256,128]{1,0:T(8,128)S(1)}, s32[1]{0:T(128)}) custom-call(s32[8]{0:T(128)} %refs_0_.2, s32[2,4]{1,0:T(2,128)} %bitcast.2), custom_call_target="tpu_custom_call" | custom-call | tf_op jit(solution)/shard_map/prepare/pallas_call | solution.py:337
  9.0 10.9 %collective-permute-done.41.refs_5_ = bf16[128,896]{1,0:T(8,128)(2,1)S(1)} collective-permute-done((bf16[128,896]{1,0:T(8,128)(2,1)S(1)}, bf16[128,896]{1,0:T(8,128)(2,1)S(1)}, u32[]{:S(2)}, u32[]{:S(2)}) %collective-permute-start.41) | collective-permute-done | bytes 229408 | tf_op jit(solution)/shard_map/ppermute | solution.py:296
  20.0 2.0 %shard_map.55 = (bf16[128,640]{1,0:T(8,128)(2,1)S(1)}, bf16[128,640]{1,0:T(8,128)(2,1)S(1)}, bf16[128,640]{1,0:T(8,128)(2,1)S(1)}, bf16[128,640]{1,0:T(8,128)(2,1)S(1)}) custom-call(s32[2,4]{1,0:T(2,128)} %bitcast.3, s32[256,128]{1,0:T(8,128)S(1)} %get-tuple-element.148.refs_1_, bf16[128,2048]{1,0:T(8,128)(2,1)S(1)} %get-tuple-element.149.refs_2_, ...), custom_call_target="tpu_custom_call" | custom-call | flops 503316480 | bytes 655360 | tf_op jit(solution)/shard_map/pallas_call | solution.py:363
  22.0 4.2 %collective-permute-start.43 = (bf16[128,640]{1,0:T(8,128)(2,1)S(1)}, bf16[128,640]{1,0:T(8,128)(2,1)S(1)}, u32[]{:S(2)}, u32[]{:S(2)}) collective-permute-start(bf16[128,640]{1,0:T(8,128)(2,1)S(1)} %get-tuple-element.153), channel_id=1, source_target_pairs={{0,0},{2,8},{4,4},{6,12},{8,2},{10,10},{12,6},{14,14},{1,1},{3,9},... | collective-permute-start | bytes 491528 | tf_op jit(solution)/shard_map/ppermute | solution.py:296
  26.2 3.1 %shard_map.56 = (bf16[128,1408]{1,0:T(8,128)(2,1)S(1)}, bf16[128,1408]{1,0:T(8,128)(2,1)S(1)}, bf16[128,1408]{1,0:T(8,128)(2,1)S(1)}, bf16[128,1408]{1,0:T(8,128)(2,1)S(1)}) custom-call(s32[2,4]{1,0:T(2,128)} %bitcast.4, s32[256,128]{1,0:T(8,128)S(1)} %get-tuple-element.148.refs_1_, bf16[128,2048]{1,0:T(8,128)(2,1)S(1)} %get-tuple-element.149.refs_2_, ...), custom_call_target="tpu_custom_call" | custom-call | flops 1107296256 | bytes 1441792 | tf_op jit(solution)/shard_map/pallas_call | solution.py:363
  29.3 26.3 %conditional.1 = (bf16[256,2816]{1,0:T(8,128)(2,1)S(1)}) conditional(s32[]{:T(128)} %bitcast.1, (bf16[128,1408]{1,0:T(8,128)(2,1)S(1)}, bf16[128,1408]{1,0:T(8,128)(2,1)S(1)}, bf16[128,1408]{1,0:T(8,128)(2,1)S(1)}, bf16[128,1408]{1,0:T(8,128)(2,1)S(1)}) %shard_map.56, (bf16[128,1408]{1,0:T(8,128)(2,1)S(1)}, ...), branch_computations={%region_0.0_spmd, %region_1.0_spmd, %region_2.0_spmd, %region_3.0_... | conditional | bytes 5767336 | solution.py:414
  29.4 2.9 %collective-permute-start = (bf16[128,1408]{1,0:T(8,128)(2,1)S(1)}, bf16[128,1408]{1,0:T(8,128)(2,1)S(1)}, u32[]{:S(2)}, u32[]{:S(2)}) collective-permute-start(bf16[128,1408]{1,0:T(8,128)(2,1)S(1)} %get-tuple-element.84), channel_id=1, source_target_pairs={{0,0},{4,4},{6,12},{8,2},{10,10},{12,6},{14,14},{1,1},{5,5},{7,13}... | collective-permute-start | bytes 1081352 | tf_op jit(solution)/shard_map/cond/branch_0_fun/ppermute | solution.py:296
  32.3 1.3 %collective-permute-start.1 = (bf16[128,1408]{1,0:T(8,128)(2,1)S(1)}, bf16[128,1408]{1,0:T(8,128)(2,1)S(1)}, u32[]{:S(2)}, u32[]{:S(2)}) collective-permute-start(bf16[128,1408]{1,0:T(8,128)(2,1)S(1)} %get-tuple-element.90), channel_id=1, source_target_pairs={{0,4},{2,12},{4,8},{6,0},{10,14},{12,10},{14,2},{1,5},{3,13},{5,9}... | collective-permute-start | bytes 1081352 | tf_op jit(solution)/shard_map/cond/branch_0_fun/ppermute | solution.py:296
  33.6 4.1 %collective-permute-start.2 = (bf16[128,1408]{1,0:T(8,128)(2,1)S(1)}, bf16[128,1408]{1,0:T(8,128)(2,1)S(1)}, u32[]{:S(2)}, u32[]{:S(2)}) collective-permute-start(bf16[128,1408]{1,0:T(8,128)(2,1)S(1)} %get-tuple-element.91), channel_id=1, source_target_pairs={{2,0},{4,12},{6,4},{8,10},{10,2},{12,14},{14,6},{3,1},{5,13},{7,5}... | collective-permute-start | bytes 1081352 | tf_op jit(solution)/shard_map/cond/branch_0_fun/ppermute | solution.py:296
  37.7 1.3 %collective-permute-start.3 = (bf16[128,1408]{1,0:T(8,128)(2,1)S(1)}, bf16[128,1408]{1,0:T(8,128)(2,1)S(1)}, u32[]{:S(2)}, u32[]{:S(2)}) collective-permute-start(bf16[128,1408]{1,0:T(8,128)(2,1)S(1)} %get-tuple-element.92), channel_id=1, source_target_pairs={{0,12},{2,4},{4,0},{6,8},{8,14},{12,2},{14,10},{1,13},{3,5},{5,1},... | collective-permute-start | bytes 1081352 | tf_op jit(solution)/shard_map/cond/branch_0_fun/ppermute | solution.py:296
  39.0 7.8 %collective-permute-done.refs_0_ = bf16[128,1408]{1,0:T(8,128)(2,1)S(1)} collective-permute-done((bf16[128,1408]{1,0:T(8,128)(2,1)S(1)}, bf16[128,1408]{1,0:T(8,128)(2,1)S(1)}, u32[]{:S(2)}, u32[]{:S(2)}) %collective-permute-start) | collective-permute-done | bytes 360480 | tf_op jit(solution)/shard_map/cond/branch_0_fun/ppermute | solution.py:296
  46.8 1.8 %collective-permute-done.1.refs_1_ = bf16[128,1408]{1,0:T(8,128)(2,1)S(1)} collective-permute-done((bf16[128,1408]{1,0:T(8,128)(2,1)S(1)}, bf16[128,1408]{1,0:T(8,128)(2,1)S(1)}, u32[]{:S(2)}, u32[]{:S(2)}) %collective-permute-start.1) | collective-permute-done | bytes 360480 | tf_op jit(solution)/shard_map/cond/branch_0_fun/ppermute | solution.py:296
  49.3 6.1 %collective-permute-done.3.refs_3_ = bf16[128,1408]{1,0:T(8,128)(2,1)S(1)} collective-permute-done((bf16[128,1408]{1,0:T(8,128)(2,1)S(1)}, bf16[128,1408]{1,0:T(8,128)(2,1)S(1)}, u32[]{:S(2)}, u32[]{:S(2)}) %collective-permute-start.3) | collective-permute-done | bytes 360480 | tf_op jit(solution)/shard_map/cond/branch_0_fun/ppermute | solution.py:296
  55.6 8.2 %collective-permute-start.44 = (bf16[128,640]{1,0:T(8,128)(2,1)S(1)}, bf16[128,640]{1,0:T(8,128)(2,1)S(1)}, u32[]{:S(2)}, u32[]{:S(2)}) collective-permute-start(bf16[128,640]{1,0:T(8,128)(2,1)S(1)} %get-tuple-element.154), channel_id=1, source_target_pairs={{0,4},{2,12},{4,8},{6,0},{8,6},{10,14},{12,10},{14,2},{1,5},{3,13}... | collective-permute-start | bytes 491528 | tf_op jit(solution)/shard_map/ppermute | solution.py:296
  63.9 3.1 %collective-permute-start.46 = (bf16[128,640]{1,0:T(8,128)(2,1)S(1)}, bf16[128,640]{1,0:T(8,128)(2,1)S(1)}, u32[]{:S(2)}, u32[]{:S(2)}) collective-permute-start(bf16[128,640]{1,0:T(8,128)(2,1)S(1)} %get-tuple-element.156), channel_id=1, source_target_pairs={{0,12},{2,4},{4,0},{6,8},{8,14},{10,6},{12,2},{14,10},{1,13},{3,5}... | collective-permute-start | bytes 491528 | tf_op jit(solution)/shard_map/ppermute | solution.py:296
  67.0 1.3 %collective-permute-done.44.refs_1_ = bf16[128,640]{1,0:T(8,128)(2,1)S(1)} collective-permute-done((bf16[128,640]{1,0:T(8,128)(2,1)S(1)}, bf16[128,640]{1,0:T(8,128)(2,1)S(1)}, u32[]{:S(2)}, u32[]{:S(2)}) %collective-permute-start.44) | collective-permute-done | bytes 163872 | tf_op jit(solution)/shard_map/ppermute | solution.py:296
  68.3 3.5 %collective-permute-done.45.refs_2_ = bf16[128,640]{1,0:T(8,128)(2,1)S(1)} collective-permute-done((bf16[128,640]{1,0:T(8,128)(2,1)S(1)}, bf16[128,640]{1,0:T(8,128)(2,1)S(1)}, u32[]{:S(2)}, u32[]{:S(2)}) %collective-permute-start.45) | collective-permute-done | bytes 163872 | tf_op jit(solution)/shard_map/ppermute | solution.py:296
  71.8 8.9 %collective-permute-done.46.refs_3_ = bf16[128,640]{1,0:T(8,128)(2,1)S(1)} collective-permute-done((bf16[128,640]{1,0:T(8,128)(2,1)S(1)}, bf16[128,640]{1,0:T(8,128)(2,1)S(1)}, u32[]{:S(2)}, u32[]{:S(2)}) %collective-permute-start.46) | collective-permute-done | bytes 163872 | tf_op jit(solution)/shard_map/ppermute | solution.py:296
  80.8 1.4 %place.1 = bf16[256,4096]{1,0:T(8,128)(2,1)} custom-call(bf16[128,640]{1,0:T(8,128)(2,1)S(1)} %collective-permute-done.43.refs_0_, bf16[128,640]{1,0:T(8,128)(2,1)S(1)} %collective-permute-done.44.refs_1_, bf16[128,640]{1,0:T(8,128)(2,1)S(1)} %collective-permute-done.45.refs_2_, bf16[128,640]{1,0:T(8,128)(2,1)S(1)} %collective-permute-done.46.refs_3_, ...), custom_call_target="tpu_custom_call" | custom-call | tf_op jit(solution)/shard_map/place/pallas_call | solution.py:418
  (9 shorter events, 1.8 us)
Async XLA Ops:
  1.5 24.7 %collective-permute-start.47 = (bf16[128,1664]{1,0:T(8,128)(2,1)S(1)}, bf16[128,1664]{1,0:T(8,128)(2,1)S(1)}, u32[]{:S(2)}, u32[]{:S(2)}) collective-permute-start(bf16[128,1664]{1,0:T(8,128)(2,1)S(1)} %get-tuple-element.158), channel_id=1, source_target_pairs={{0,2},{2,0},{4,6},{6,4},{8,10},{10,8},{12,14},{14,12},{1,3},{3,1},... | collective-permute-start | bytes 1277960 | tf_op jit(solution)/shard_map/ppermute | solution.py:296
  1.8 18.2 %collective-permute-start.41 = (bf16[128,896]{1,0:T(8,128)(2,1)S(1)}, bf16[128,896]{1,0:T(8,128)(2,1)S(1)}, u32[]{:S(2)}, u32[]{:S(2)}) collective-permute-start(bf16[128,896]{1,0:T(8,128)(2,1)S(1)} %get-tuple-element.151), channel_id=1, source_target_pairs={{0,2},{2,0},{4,6},{6,4},{8,10},{10,8},{12,14},{14,12},{1,3},{3,1},... | collective-permute-start | bytes 688136 | tf_op jit(solution)/shard_map/ppermute | solution.py:296
  3.0 6.0 %collective-permute-start.40 = (bf16[128,512]{1,0:T(8,128)(2,1)S(1)}, bf16[128,512]{1,0:T(8,128)(2,1)S(1)}, u32[]{:S(2)}, u32[]{:S(2)}) collective-permute-start(bf16[128,512]{1,0:T(8,128)(2,1)S(1)} %get-tuple-element.150.refs_3_), channel_id=1, source_target_pairs={{0,4},{2,6},{4,8},{6,10},{8,12},{10,14},{12,0},{14,2},{1,5},{3,7},... | collective-permute-start | bytes 393224 | tf_op jit(solution)/shard_map/ppermute | solution.py:296
  4.3 4.7 %collective-permute-start.42 = (bf16[128,256]{1,0:T(8,128)(2,1)S(1)}, bf16[128,256]{1,0:T(8,128)(2,1)S(1)}, u32[]{:S(2)}, u32[]{:S(2)}) collective-permute-start(bf16[128,256]{1,0:T(8,128)(2,1)S(1)} %get-tuple-element.152), channel_id=1, source_target_pairs={{0,6},{2,4},{4,10},{6,8},{8,14},{10,12},{12,2},{14,0},{1,7},{3,5},... | collective-permute-start | bytes 196616 | tf_op jit(solution)/shard_map/ppermute | solution.py:296
  5.6 20.6 %collective-permute-start.48 = (bf16[128,256]{1,0:T(8,128)(2,1)S(1)}, bf16[128,256]{1,0:T(8,128)(2,1)S(1)}, u32[]{:S(2)}, u32[]{:S(2)}) collective-permute-start(bf16[128,256]{1,0:T(8,128)(2,1)S(1)} %get-tuple-element.159), channel_id=1, source_target_pairs={{0,6},{2,4},{4,10},{6,8},{8,14},{10,12},{12,2},{14,0},{1,7},{3,5},... | collective-permute-start | bytes 196616 | tf_op jit(solution)/shard_map/ppermute | solution.py:296
  22.0 45.0 %collective-permute-start.43 = (bf16[128,640]{1,0:T(8,128)(2,1)S(1)}, bf16[128,640]{1,0:T(8,128)(2,1)S(1)}, u32[]{:S(2)}, u32[]{:S(2)}) collective-permute-start(bf16[128,640]{1,0:T(8,128)(2,1)S(1)} %get-tuple-element.153), channel_id=1, source_target_pairs={{0,0},{2,8},{4,4},{6,12},{8,2},{10,10},{12,6},{14,14},{1,1},{3,9},... | collective-permute-start | bytes 491528 | tf_op jit(solution)/shard_map/ppermute | solution.py:296
  29.4 17.4 %collective-permute-start = (bf16[128,1408]{1,0:T(8,128)(2,1)S(1)}, bf16[128,1408]{1,0:T(8,128)(2,1)S(1)}, u32[]{:S(2)}, u32[]{:S(2)}) collective-permute-start(bf16[128,1408]{1,0:T(8,128)(2,1)S(1)} %get-tuple-element.84), channel_id=1, source_target_pairs={{0,0},{4,4},{6,12},{8,2},{10,10},{12,6},{14,14},{1,1},{5,5},{7,13}... | collective-permute-start | bytes 1081352 | tf_op jit(solution)/shard_map/cond/branch_0_fun/ppermute | solution.py:296
  32.3 16.3 %collective-permute-start.1 = (bf16[128,1408]{1,0:T(8,128)(2,1)S(1)}, bf16[128,1408]{1,0:T(8,128)(2,1)S(1)}, u32[]{:S(2)}, u32[]{:S(2)}) collective-permute-start(bf16[128,1408]{1,0:T(8,128)(2,1)S(1)} %get-tuple-element.90), channel_id=1, source_target_pairs={{0,4},{2,12},{4,8},{6,0},{10,14},{12,10},{14,2},{1,5},{3,13},{5,9}... | collective-permute-start | bytes 1081352 | tf_op jit(solution)/shard_map/cond/branch_0_fun/ppermute | solution.py:296
  33.6 15.7 %collective-permute-start.2 = (bf16[128,1408]{1,0:T(8,128)(2,1)S(1)}, bf16[128,1408]{1,0:T(8,128)(2,1)S(1)}, u32[]{:S(2)}, u32[]{:S(2)}) collective-permute-start(bf16[128,1408]{1,0:T(8,128)(2,1)S(1)} %get-tuple-element.91), channel_id=1, source_target_pairs={{2,0},{4,12},{6,4},{8,10},{10,2},{12,14},{14,6},{3,1},{5,13},{7,5}... | collective-permute-start | bytes 1081352 | tf_op jit(solution)/shard_map/cond/branch_0_fun/ppermute | solution.py:296
  37.7 17.7 %collective-permute-start.3 = (bf16[128,1408]{1,0:T(8,128)(2,1)S(1)}, bf16[128,1408]{1,0:T(8,128)(2,1)S(1)}, u32[]{:S(2)}, u32[]{:S(2)}) collective-permute-start(bf16[128,1408]{1,0:T(8,128)(2,1)S(1)} %get-tuple-element.92), channel_id=1, source_target_pairs={{0,12},{2,4},{4,0},{6,8},{8,14},{12,2},{14,10},{1,13},{3,5},{5,1},... | collective-permute-start | bytes 1081352 | tf_op jit(solution)/shard_map/cond/branch_0_fun/ppermute | solution.py:296
  55.6 12.7 %collective-permute-start.44 = (bf16[128,640]{1,0:T(8,128)(2,1)S(1)}, bf16[128,640]{1,0:T(8,128)(2,1)S(1)}, u32[]{:S(2)}, u32[]{:S(2)}) collective-permute-start(bf16[128,640]{1,0:T(8,128)(2,1)S(1)} %get-tuple-element.154), channel_id=1, source_target_pairs={{0,4},{2,12},{4,8},{6,0},{8,6},{10,14},{12,10},{14,2},{1,5},{3,13}... | collective-permute-start | bytes 491528 | tf_op jit(solution)/shard_map/ppermute | solution.py:296
  63.8 8.0 %collective-permute-start.45 = (bf16[128,640]{1,0:T(8,128)(2,1)S(1)}, bf16[128,640]{1,0:T(8,128)(2,1)S(1)}, u32[]{:S(2)}, u32[]{:S(2)}) collective-permute-start(bf16[128,640]{1,0:T(8,128)(2,1)S(1)} %get-tuple-element.155), channel_id=1, source_target_pairs={{0,8},{2,0},{4,12},{6,4},{8,10},{10,2},{12,14},{14,6},{1,9},{3,1},... | collective-permute-start | bytes 491528 | tf_op jit(solution)/shard_map/ppermute | solution.py:296
  63.9 16.9 %collective-permute-start.46 = (bf16[128,640]{1,0:T(8,128)(2,1)S(1)}, bf16[128,640]{1,0:T(8,128)(2,1)S(1)}, u32[]{:S(2)}, u32[]{:S(2)}) collective-permute-start(bf16[128,640]{1,0:T(8,128)(2,1)S(1)} %get-tuple-element.156), channel_id=1, source_target_pairs={{0,12},{2,4},{4,0},{6,8},{8,14},{10,6},{12,2},{14,10},{1,13},{3,5}... | collective-permute-start | bytes 491528 | tf_op jit(solution)/shard_map/ppermute | solution.py:296

commit v4 on v3

--- a/solution.py
+++ b/solution.py
@@ -57,7 +57,7 @@
     low, high = range(half), range(half, seq_count)
     up = [(group, owner) for group in low for owner in high]
     down = [(group, owner) for group in high for owner in low]
-    order = ((0, 1), (0, 2), (0, 3), (1, 2), (1, 3), (2, 0), (2, 3), (3, 0), (3, 1))
+    order = ((1, 2), (3, 0), (3, 2), (0, 3), (0, 2), (1, 0), (2, 2), (1, 3), (2, 1))
     return [(up[u], down[d]) for u, d in order]
 
 
@@ -135,14 +135,16 @@
 def attend_kernel(seq_count, block_axis, pair_room, kv_width, chunks, index, *refs):
     refs = list(refs)
     take = lambda count: [refs.pop(0) for _ in range(count)]
-    plan_ref, start_ref, own_query, own_kv, straight = take(5)
+    plan_hbm, start_ref, own_query, own_kv, straight = take(5)
     home_refs, cross_refs = [], []
     for came in range(index + 1):
         low, high = new_kv(chunks, came)
         home_refs.append(take(block_axis - 1))
         cross_refs.append(take(block_axis - 1 if high > low else 0))
     message_refs = take(seq_count)
-    query_all, key_all, value_all, result = refs
+    query_all, key_all, value_all, result, plan_ref, plan_sem = refs
+    plan_copy = pltpu.make_async_copy(plan_hbm, plan_ref, plan_sem)
+    plan_copy.start()
     group = lax.axis_index("seq")
     blk = lax.axis_index("blk")
     group_len = block_axis * BLOCK
@@ -220,6 +222,7 @@
         return carried
 
     lax.fori_loop(0, block_axis, attend, 0)
+    plan_copy.wait()
 
     for step in range(seq_count):
         owner = owner_of(step, group, blk, seq_count, block_axis)
@@ -365,13 +368,15 @@
                 seq_count, block_axis, pair_room, kv_width, chunks, index, *refs
             ),
             out_shape=[bf16(slot_rows, width)] * seq_count,
-            in_specs=[smem] + [vmem] * len(inputs),
+            in_specs=[hbm] + [vmem] * len(inputs),
             out_specs=[vmem] * seq_count,
             scratch_shapes=[
                 pltpu.VMEM((block_axis, heads * BLOCK, HEAD_WIDTH), jnp.bfloat16),
                 pltpu.VMEM((2 * block_axis * BLOCK, kv_span), jnp.bfloat16),
                 pltpu.VMEM((2 * block_axis * BLOCK, kv_span), jnp.bfloat16),
                 pltpu.VMEM((block_axis, BLOCK, width), jnp.bfloat16),
+                pltpu.SMEM(plan.shape, jnp.int32),
+                pltpu.SemaphoreType.DMA,
             ],
             cost_estimate=pl.CostEstimate(
                 flops=8 * group_blocks * BLOCK * window * width,

time: 82.4 us -> 79.4 us (0.964)
  the two profiles are of different devices: /device:TPU:11 before, /device:TPU:10 now
where the time goes in v4:
time: 79.4 us; the launch traced here: 79.2 us
  waiting for transfers between devices  44.9 us (57%)
  starting transfers between devices  25.2 us (32%)
  Pallas kernels  8.28 us (10%)
    ppermute x13, waiting for transfers between devices, permute(): return lax.ppermute(array, ('seq', 'blk'), pairs)  44.9 us
    ppermute x13, starting transfers between devices, permute(): return lax.ppermute(array, ('seq', 'blk'), pairs)  25.2 us
    pallas_call x2, Pallas kernels, attend(): pl.pallas_call(lambda *refs: attend_kernel(seq_count, block_axis, pair_ro...  3.83 us
  transfers between devices with their start and end apart: 13, of which 6 were waited for; matrix products, arithmetic and copies ran while one was open for 0% of the time, Pallas kernels for 7%

profile of v4, /device:TPU:10, one launch (start us, length us, event | category | flops | bytes accessed | tf_op | source)
XLA Modules:
  0.0 79.2 jit_solution(14435154571983957760)
XLA Ops:
  0.0 1.5 %pack.1 = (bf16[128,2048]{1,0:T(8,128)(2,1)S(1)}, bf16[128,512]{1,0:T(8,128)(2,1)S(1)}, bf16[128,896]{1,0:T(8,128)(2,1)S(1)}, bf16[128,256]{1,0:T(8,128)(2,1)S(1...) custom-call(bf16[128,4096]{1,0:T(8,128)(2,1)} %refs_0_.3, bf16[128,512]{1,0:T(8,128)(2,1)} %refs_1_.1, ...), custom_call_target="tpu_custom_call" | custom-call | tf_op jit(solution)/shard_map/pack/pallas_call | solution.py:317
  1.5 0.6 collective-permute-start.47
  2.1 1.5 %collective-permute-start.41 = (bf16[128,896]{1,0:T(8,128)(2,1)S(1)}, bf16[128,896]{1,0:T(8,128)(2,1)S(1)}, u32[]{:S(2)}, u32[]{:S(2)}) collective-permute-start(bf16[128,896]{1,0:T(8,128)(2,1)S(1)} %get-tuple-element.151), channel_id=1, source_target_pairs={{0,2},{2,0},{4,6},{6,4},{8,10},{10,8},{12,14},{14,12},{1,3},{3,1},... | collective-permute-start | bytes 688136 | tf_op jit(solution)/shard_map/ppermute | solution.py:299
  3.6 1.6 %collective-permute-start.40 = (bf16[128,512]{1,0:T(8,128)(2,1)S(1)}, bf16[128,512]{1,0:T(8,128)(2,1)S(1)}, u32[]{:S(2)}, u32[]{:S(2)}) collective-permute-start(bf16[128,512]{1,0:T(8,128)(2,1)S(1)} %get-tuple-element.150.refs_3_), channel_id=1, source_target_pairs={{0,4},{2,6},{4,8},{6,10},{8,12},{10,14},{12,0},{14,2},{1,5},{3,7},... | collective-permute-start | bytes 393224 | tf_op jit(solution)/shard_map/ppermute | solution.py:299
  5.1 1.5 %collective-permute-start.42 = (bf16[128,256]{1,0:T(8,128)(2,1)S(1)}, bf16[128,256]{1,0:T(8,128)(2,1)S(1)}, u32[]{:S(2)}, u32[]{:S(2)}) collective-permute-start(bf16[128,256]{1,0:T(8,128)(2,1)S(1)} %get-tuple-element.152), channel_id=1, source_target_pairs={{0,6},{2,4},{4,10},{6,8},{8,14},{10,12},{12,2},{14,0},{1,7},{3,5},... | collective-permute-start | bytes 196616 | tf_op jit(solution)/shard_map/ppermute | solution.py:299
  6.7 1.1 %collective-permute-start.48 = (bf16[128,256]{1,0:T(8,128)(2,1)S(1)}, bf16[128,256]{1,0:T(8,128)(2,1)S(1)}, u32[]{:S(2)}, u32[]{:S(2)}) collective-permute-start(bf16[128,256]{1,0:T(8,128)(2,1)S(1)} %get-tuple-element.159), channel_id=1, source_target_pairs={{0,6},{2,4},{4,10},{6,8},{8,14},{10,12},{12,2},{14,0},{1,7},{3,5},... | collective-permute-start | bytes 196616 | tf_op jit(solution)/shard_map/ppermute | solution.py:299
  7.8 1.4 %prepare.1 = (s32[256,128]{1,0:T(8,128)S(1)}, s32[1]{0:T(128)}) custom-call(s32[8]{0:T(128)} %refs_0_.2, s32[2,4]{1,0:T(2,128)} %bitcast.2), custom_call_target="tpu_custom_call" | custom-call | tf_op jit(solution)/shard_map/prepare/pallas_call | solution.py:340
  9.9 0.8 collective-permute-done.42.refs_6_
  10.7 10.1 %collective-permute-done.41.refs_5_ = bf16[128,896]{1,0:T(8,128)(2,1)S(1)} collective-permute-done((bf16[128,896]{1,0:T(8,128)(2,1)S(1)}, bf16[128,896]{1,0:T(8,128)(2,1)S(1)}, u32[]{:S(2)}, u32[]{:S(2)}) %collective-permute-start.41) | collective-permute-done | bytes 229408 | tf_op jit(solution)/shard_map/ppermute | solution.py:299
  20.8 1.4 %shard_map.55 = (bf16[128,640]{1,0:T(8,128)(2,1)S(1)}, bf16[128,640]{1,0:T(8,128)(2,1)S(1)}, bf16[128,640]{1,0:T(8,128)(2,1)S(1)}, bf16[128,640]{1,0:T(8,128)(2,1)S(1)}) custom-call(s32[2,4]{1,0:T(2,128)} %bitcast.3, s32[256,128]{1,0:T(8,128)S(1)} %get-tuple-element.148.refs_1_, bf16[128,2048]{1,0:T(8,128)(2,1)S(1)} %get-tuple-element.149.refs_2_, ...), custom_call_target="tpu_custom_call" | custom-call | flops 503316480 | bytes 655360 | tf_op jit(solution)/shard_map/pallas_call | solution.py:366
  22.2 4.5 %collective-permute-start.43 = (bf16[128,640]{1,0:T(8,128)(2,1)S(1)}, bf16[128,640]{1,0:T(8,128)(2,1)S(1)}, u32[]{:S(2)}, u32[]{:S(2)}) collective-permute-start(bf16[128,640]{1,0:T(8,128)(2,1)S(1)} %get-tuple-element.153), channel_id=1, source_target_pairs={{0,0},{2,8},{4,4},{6,12},{8,2},{10,10},{12,6},{14,14},{1,1},{3,9},... | collective-permute-start | bytes 491528 | tf_op jit(solution)/shard_map/ppermute | solution.py:299
  26.7 2.5 %shard_map.56 = (bf16[128,1408]{1,0:T(8,128)(2,1)S(1)}, bf16[128,1408]{1,0:T(8,128)(2,1)S(1)}, bf16[128,1408]{1,0:T(8,128)(2,1)S(1)}, bf16[128,1408]{1,0:T(8,128)(2,1)S(1)}) custom-call(s32[2,4]{1,0:T(2,128)} %bitcast.4, s32[256,128]{1,0:T(8,128)S(1)} %get-tuple-element.148.refs_1_, bf16[128,2048]{1,0:T(8,128)(2,1)S(1)} %get-tuple-element.149.refs_2_, ...), custom_call_target="tpu_custom_call" | custom-call | flops 1107296256 | bytes 1441792 | tf_op jit(solution)/shard_map/pallas_call | solution.py:366
  29.2 26.9 %conditional.1 = (bf16[256,2816]{1,0:T(8,128)(2,1)S(1)}) conditional(s32[]{:T(128)} %bitcast.1, (bf16[128,1408]{1,0:T(8,128)(2,1)S(1)}, bf16[128,1408]{1,0:T(8,128)(2,1)S(1)}, bf16[128,1408]{1,0:T(8,128)(2,1)S(1)}, bf16[128,1408]{1,0:T(8,128)(2,1)S(1)}) %shard_map.56, (bf16[128,1408]{1,0:T(8,128)(2,1)S(1)}, ...), branch_computations={%region_0.0_spmd, %region_1.0_spmd, %region_2.0_spmd, %region_3.0_... | conditional | bytes 5767336 | solution.py:419
  29.2 3.2 %collective-permute-start.32 = (bf16[128,1408]{1,0:T(8,128)(2,1)S(1)}, bf16[128,1408]{1,0:T(8,128)(2,1)S(1)}, u32[]{:S(2)}, u32[]{:S(2)}) collective-permute-start(bf16[128,1408]{1,0:T(8,128)(2,1)S(1)} %get-tuple-element.128), channel_id=1, source_target_pairs={{0,0},{2,8},{4,4},{6,12},{8,2},{10,10},{12,6},{14,14},{1,1},{3,9},... | collective-permute-start | bytes 1081352 | tf_op jit(solution)/shard_map/cond/branch_8_fun/ppermute | solution.py:299
  32.4 1.3 %collective-permute-start.33 = (bf16[128,1408]{1,0:T(8,128)(2,1)S(1)}, bf16[128,1408]{1,0:T(8,128)(2,1)S(1)}, u32[]{:S(2)}, u32[]{:S(2)}) collective-permute-start(bf16[128,1408]{1,0:T(8,128)(2,1)S(1)} %get-tuple-element.129), channel_id=1, source_target_pairs={{0,4},{2,12},{6,0},{10,14},{12,10},{14,2},{1,5},{3,13},{7,1},{11,1... | collective-permute-start | bytes 1081352 | tf_op jit(solution)/shard_map/cond/branch_8_fun/ppermute | solution.py:299
  33.8 0.7 collective-permute-start.35
  34.5 21.4 %collective-permute-done.32.refs_0_ = bf16[128,1408]{1,0:T(8,128)(2,1)S(1)} collective-permute-done((bf16[128,1408]{1,0:T(8,128)(2,1)S(1)}, bf16[128,1408]{1,0:T(8,128)(2,1)S(1)}, u32[]{:S(2)}, u32[]{:S(2)}) %collective-permute-start.32) | collective-permute-done | bytes 360480 | tf_op jit(solution)/shard_map/cond/branch_8_fun/ppermute | solution.py:299
  55.9 0.2 gather.18
  56.1 6.3 %collective-permute-start.44 = (bf16[128,640]{1,0:T(8,128)(2,1)S(1)}, bf16[128,640]{1,0:T(8,128)(2,1)S(1)}, u32[]{:S(2)}, u32[]{:S(2)}) collective-permute-start(bf16[128,640]{1,0:T(8,128)(2,1)S(1)} %get-tuple-element.154), channel_id=1, source_target_pairs={{0,4},{2,12},{4,8},{6,0},{8,6},{10,14},{12,10},{14,2},{1,5},{3,13}... | collective-permute-start | bytes 491528 | tf_op jit(solution)/shard_map/ppermute | solution.py:299
  62.4 2.8 %collective-permute-start.46 = (bf16[128,640]{1,0:T(8,128)(2,1)S(1)}, bf16[128,640]{1,0:T(8,128)(2,1)S(1)}, u32[]{:S(2)}, u32[]{:S(2)}) collective-permute-start(bf16[128,640]{1,0:T(8,128)(2,1)S(1)} %get-tuple-element.156), channel_id=1, source_target_pairs={{0,12},{2,4},{4,0},{6,8},{8,14},{10,6},{12,2},{14,10},{1,13},{3,5}... | collective-permute-start | bytes 491528 | tf_op jit(solution)/shard_map/ppermute | solution.py:299
  65.2 3.1 %collective-permute-done.44.refs_1_ = bf16[128,640]{1,0:T(8,128)(2,1)S(1)} collective-permute-done((bf16[128,640]{1,0:T(8,128)(2,1)S(1)}, bf16[128,640]{1,0:T(8,128)(2,1)S(1)}, u32[]{:S(2)}, u32[]{:S(2)}) %collective-permute-start.44) | collective-permute-done | bytes 163872 | tf_op jit(solution)/shard_map/ppermute | solution.py:299
  68.3 3.7 %collective-permute-done.45.refs_2_ = bf16[128,640]{1,0:T(8,128)(2,1)S(1)} collective-permute-done((bf16[128,640]{1,0:T(8,128)(2,1)S(1)}, bf16[128,640]{1,0:T(8,128)(2,1)S(1)}, u32[]{:S(2)}, u32[]{:S(2)}) %collective-permute-start.45) | collective-permute-done | bytes 163872 | tf_op jit(solution)/shard_map/ppermute | solution.py:299
  72.0 5.8 %collective-permute-done.46.refs_3_ = bf16[128,640]{1,0:T(8,128)(2,1)S(1)} collective-permute-done((bf16[128,640]{1,0:T(8,128)(2,1)S(1)}, bf16[128,640]{1,0:T(8,128)(2,1)S(1)}, u32[]{:S(2)}, u32[]{:S(2)}) %collective-permute-start.46) | collective-permute-done | bytes 163872 | tf_op jit(solution)/shard_map/ppermute | solution.py:299
  77.8 1.4 %place.1 = bf16[256,4096]{1,0:T(8,128)(2,1)} custom-call(bf16[128,640]{1,0:T(8,128)(2,1)S(1)} %collective-permute-done.43.refs_0_, bf16[128,640]{1,0:T(8,128)(2,1)S(1)} %collective-permute-done.44.refs_1_, bf16[128,640]{1,0:T(8,128)(2,1)S(1)} %collective-permute-done.45.refs_2_, bf16[128,640]{1,0:T(8,128)(2,1)S(1)} %collective-permute-done.46.refs_3_, ...), custom_call_target="tpu_custom_call" | custom-call | tf_op jit(solution)/shard_map/place/pallas_call | solution.py:423
  (9 shorter events, 0.1 us)
Async XLA Ops:
  1.5 25.2 %collective-permute-start.47 = (bf16[128,1664]{1,0:T(8,128)(2,1)S(1)}, bf16[128,1664]{1,0:T(8,128)(2,1)S(1)}, u32[]{:S(2)}, u32[]{:S(2)}) collective-permute-start(bf16[128,1664]{1,0:T(8,128)(2,1)S(1)} %get-tuple-element.158), channel_id=1, source_target_pairs={{0,2},{2,0},{4,6},{6,4},{8,10},{10,8},{12,14},{14,12},{1,3},{3,1},... | collective-permute-start | bytes 1277960 | tf_op jit(solution)/shard_map/ppermute | solution.py:299
  2.1 18.7 %collective-permute-start.41 = (bf16[128,896]{1,0:T(8,128)(2,1)S(1)}, bf16[128,896]{1,0:T(8,128)(2,1)S(1)}, u32[]{:S(2)}, u32[]{:S(2)}) collective-permute-start(bf16[128,896]{1,0:T(8,128)(2,1)S(1)} %get-tuple-element.151), channel_id=1, source_target_pairs={{0,2},{2,0},{4,6},{6,4},{8,10},{10,8},{12,14},{14,12},{1,3},{3,1},... | collective-permute-start | bytes 688136 | tf_op jit(solution)/shard_map/ppermute | solution.py:299
  3.6 7.2 %collective-permute-start.40 = (bf16[128,512]{1,0:T(8,128)(2,1)S(1)}, bf16[128,512]{1,0:T(8,128)(2,1)S(1)}, u32[]{:S(2)}, u32[]{:S(2)}) collective-permute-start(bf16[128,512]{1,0:T(8,128)(2,1)S(1)} %get-tuple-element.150.refs_3_), channel_id=1, source_target_pairs={{0,4},{2,6},{4,8},{6,10},{8,12},{10,14},{12,0},{14,2},{1,5},{3,7},... | collective-permute-start | bytes 393224 | tf_op jit(solution)/shard_map/ppermute | solution.py:299
  5.1 5.6 %collective-permute-start.42 = (bf16[128,256]{1,0:T(8,128)(2,1)S(1)}, bf16[128,256]{1,0:T(8,128)(2,1)S(1)}, u32[]{:S(2)}, u32[]{:S(2)}) collective-permute-start(bf16[128,256]{1,0:T(8,128)(2,1)S(1)} %get-tuple-element.152), channel_id=1, source_target_pairs={{0,6},{2,4},{4,10},{6,8},{8,14},{10,12},{12,2},{14,0},{1,7},{3,5},... | collective-permute-start | bytes 196616 | tf_op jit(solution)/shard_map/ppermute | solution.py:299
  6.7 20.0 %collective-permute-start.48 = (bf16[128,256]{1,0:T(8,128)(2,1)S(1)}, bf16[128,256]{1,0:T(8,128)(2,1)S(1)}, u32[]{:S(2)}, u32[]{:S(2)}) collective-permute-start(bf16[128,256]{1,0:T(8,128)(2,1)S(1)} %get-tuple-element.159), channel_id=1, source_target_pairs={{0,6},{2,4},{4,10},{6,8},{8,14},{10,12},{12,2},{14,0},{1,7},{3,5},... | collective-permute-start | bytes 196616 | tf_op jit(solution)/shard_map/ppermute | solution.py:299
  22.2 43.0 %collective-permute-start.43 = (bf16[128,640]{1,0:T(8,128)(2,1)S(1)}, bf16[128,640]{1,0:T(8,128)(2,1)S(1)}, u32[]{:S(2)}, u32[]{:S(2)}) collective-permute-start(bf16[128,640]{1,0:T(8,128)(2,1)S(1)} %get-tuple-element.153), channel_id=1, source_target_pairs={{0,0},{2,8},{4,4},{6,12},{8,2},{10,10},{12,6},{14,14},{1,1},{3,9},... | collective-permute-start | bytes 491528 | tf_op jit(solution)/shard_map/ppermute | solution.py:299
  29.2 26.7 %collective-permute-start.32 = (bf16[128,1408]{1,0:T(8,128)(2,1)S(1)}, bf16[128,1408]{1,0:T(8,128)(2,1)S(1)}, u32[]{:S(2)}, u32[]{:S(2)}) collective-permute-start(bf16[128,1408]{1,0:T(8,128)(2,1)S(1)} %get-tuple-element.128), channel_id=1, source_target_pairs={{0,0},{2,8},{4,4},{6,12},{8,2},{10,10},{12,6},{14,14},{1,1},{3,9},... | collective-permute-start | bytes 1081352 | tf_op jit(solution)/shard_map/cond/branch_8_fun/ppermute | solution.py:299
  32.4 23.5 %collective-permute-start.33 = (bf16[128,1408]{1,0:T(8,128)(2,1)S(1)}, bf16[128,1408]{1,0:T(8,128)(2,1)S(1)}, u32[]{:S(2)}, u32[]{:S(2)}) collective-permute-start(bf16[128,1408]{1,0:T(8,128)(2,1)S(1)} %get-tuple-element.129), channel_id=1, source_target_pairs={{0,4},{2,12},{6,0},{10,14},{12,10},{14,2},{1,5},{3,13},{7,1},{11,1... | collective-permute-start | bytes 1081352 | tf_op jit(solution)/shard_map/cond/branch_8_fun/ppermute | solution.py:299
  33.7 22.2 %collective-permute-start.34 = (bf16[128,1408]{1,0:T(8,128)(2,1)S(1)}, bf16[128,1408]{1,0:T(8,128)(2,1)S(1)}, u32[]{:S(2)}, u32[]{:S(2)}) collective-permute-start(bf16[128,1408]{1,0:T(8,128)(2,1)S(1)} %get-tuple-element.130), channel_id=1, source_target_pairs={{0,8},{2,0},{4,12},{6,4},{8,10},{10,2},{12,14},{14,6},{1,9},{3,1},... | collective-permute-start | bytes 1081352 | tf_op jit(solution)/shard_map/cond/branch_8_fun/ppermute | solution.py:299
  33.8 22.1 %collective-permute-start.35 = (bf16[128,1408]{1,0:T(8,128)(2,1)S(1)}, bf16[128,1408]{1,0:T(8,128)(2,1)S(1)}, u32[]{:S(2)}, u32[]{:S(2)}) collective-permute-start(bf16[128,1408]{1,0:T(8,128)(2,1)S(1)} %get-tuple-element.131), channel_id=1, source_target_pairs={{0,12},{2,4},{4,0},{8,14},{12,2},{14,10},{1,13},{3,5},{5,1},{9,15}... | collective-permute-start | bytes 1081352 | tf_op jit(solution)/shard_map/cond/branch_8_fun/ppermute | solution.py:299
  56.1 12.2 %collective-permute-start.44 = (bf16[128,640]{1,0:T(8,128)(2,1)S(1)}, bf16[128,640]{1,0:T(8,128)(2,1)S(1)}, u32[]{:S(2)}, u32[]{:S(2)}) collective-permute-start(bf16[128,640]{1,0:T(8,128)(2,1)S(1)} %get-tuple-element.154), channel_id=1, source_target_pairs={{0,4},{2,12},{4,8},{6,0},{8,6},{10,14},{12,10},{14,2},{1,5},{3,13}... | collective-permute-start | bytes 491528 | tf_op jit(solution)/shard_map/ppermute | solution.py:299
  62.4 9.6 %collective-permute-start.45 = (bf16[128,640]{1,0:T(8,128)(2,1)S(1)}, bf16[128,640]{1,0:T(8,128)(2,1)S(1)}, u32[]{:S(2)}, u32[]{:S(2)}) collective-permute-start(bf16[128,640]{1,0:T(8,128)(2,1)S(1)} %get-tuple-element.155), channel_id=1, source_target_pairs={{0,8},{2,0},{4,12},{6,4},{8,10},{10,2},{12,14},{14,6},{1,9},{3,1},... | collective-permute-start | bytes 491528 | tf_op jit(solution)/shard_map/ppermute | solution.py:299
  62.4 15.4 %collective-permute-start.46 = (bf16[128,640]{1,0:T(8,128)(2,1)S(1)}, bf16[128,640]{1,0:T(8,128)(2,1)S(1)}, u32[]{:S(2)}, u32[]{:S(2)}) collective-permute-start(bf16[128,640]{1,0:T(8,128)(2,1)S(1)} %get-tuple-element.156), channel_id=1, source_target_pairs={{0,12},{2,4},{4,0},{6,8},{8,14},{10,6},{12,2},{14,10},{1,13},{3,5}... | collective-permute-start | bytes 491528 | tf_op jit(solution)/shard_map/ppermute | solution.py:299
